TPU v7x, 8 devices: a whole 2x2x1 slice. The times are simulated.
8 devices in a mesh: layer: 1 (over z), col: 2 (over y), row: 4 (over x, core).
Axes of the slice: x: 2, y: 2, z: 1, core: 2. Of those that a mesh axis runs over, the one named last changes fastest.
Arguments:
- weight: float32 [1024, 4096], P(('layer', 'row'), 'col')
- grad_in: float32 [1024, 4096], P(('layer', 'row'), 'col')
- mom_first: float32 [1024, 4096], P(('layer', 'row'), 'col')
- mom_second: float32 [1024, 4096], P(('layer', 'row'), 'col')
- stat_left: float32 [1024, 1024], P(('layer', 'row'), 'col')
- stat_right: float32 [4096, 4096], P(('layer', 'row'), 'col')
- basis_left: float32 [1024, 1024], P(('layer', 'row'), 'col')
- basis_right: float32 [4096, 4096], P(('layer', 'row'), 'col')
Outputs:
- output 1: float32 [1024, 4096], P(('layer', 'row'), 'col')
- output 2: float32 [1024, 4096], P(('layer', 'row'), 'col')
- output 3: float32 [1024, 4096], P(('layer', 'row'), 'col')
- output 4: float32 [1024, 1024], P(('layer', 'row'), 'col')
- output 5: float32 [4096, 4096], P(('layer', 'row'), 'col')
All inputs are finite; a program needn't handle non-finite values.
Results may differ from a plain program's by a relative error of at most 0.001.
Values are sent between devices in bfloat16 or wider.
A program may use at most 1 GiB of HBM per device.

v0:
```python
import jax
import jax.numpy as jnp
from jax import lax
from jax.sharding import PartitionSpec as P

BETA1 = 0.9
BETA2 = 0.9
EPS = 1e-8
LR = 0.1
STEP = 10
BIAS_ONE = 1.0 - BETA1 ** STEP
BIAS_TWO = 1.0 - BETA2 ** STEP


def solution(mesh):
    tile_spec = P(("layer", "row"), "col")
    highest = lax.Precision.HIGHEST
    contract_rows = (((0,), (0,)), ((), ()))
    contract_cols = (((1,), (1,)), ((), ()))

    def local_step(weight, grad_in, mom_first, mom_second, stat_left, stat_right, basis_left, basis_right):
        grad_rows = lax.all_gather(grad_in, "col", axis=1, tiled=True)
        grad_cols = lax.all_gather(grad_in, "row", axis=0, tiled=True)
        left_part = lax.dot_general(grad_in, grad_cols, contract_cols, precision=highest, preferred_element_type=jnp.float32)
        left_sum = lax.psum_scatter(left_part, "col", scatter_dimension=1, tiled=True)
        right_part = lax.dot_general(grad_rows, grad_in, contract_rows, precision=highest, preferred_element_type=jnp.float32)
        right_sum = lax.psum_scatter(right_part, "row", scatter_dimension=0, tiled=True)
        new_left = BETA2 * stat_left + (1.0 - BETA2) * left_sum
        new_right = BETA2 * stat_right + (1.0 - BETA2) * right_sum
        left_rows = lax.all_gather(basis_left.astype(jnp.bfloat16), "col", axis=1, tiled=True)
        right_cols = lax.all_gather(basis_right.astype(jnp.bfloat16), "row", axis=0, tiled=True)
        inner_rot = jnp.dot(grad_rows.astype(jnp.bfloat16), right_cols, preferred_element_type=jnp.float32).astype(jnp.bfloat16)
        rotated_part = lax.dot_general(left_rows, inner_rot, contract_rows, preferred_element_type=jnp.float32)
        rotated = lax.psum_scatter(rotated_part, "row", scatter_dimension=0, tiled=True)
        new_first = BETA1 * mom_first + (1.0 - BETA1) * rotated
        new_second = BETA2 * mom_second + (1.0 - BETA2) * rotated * rotated
        direction = (new_first / BIAS_ONE) / (jnp.sqrt(new_second / BIAS_TWO) + EPS)
        direction_cols = lax.all_gather(direction.astype(jnp.bfloat16), "row", axis=0, tiled=True)
        back_inner = jnp.dot(left_rows, direction_cols, preferred_element_type=jnp.float32).astype(jnp.bfloat16)
        update_part = lax.dot_general(back_inner, right_cols, contract_cols, preferred_element_type=jnp.float32)
        step_update = lax.psum_scatter(update_part, "col", scatter_dimension=1, tiled=True)
        new_weight = weight - LR * step_update
        return new_weight, new_first, new_second, new_left, new_right

    return jax.shard_map(local_step, mesh=mesh, in_specs=(tile_spec,) * 8, out_specs=(tile_spec,) * 5, check_vma=False)
```

profile of v0, /device:TPU:0, one launch (start us, length us, event | category | flops | bytes accessed | tf_op | source)
XLA Modules:
  0.0 672.6 jit_solution(17485934095150506968)
XLA Ops:
  7.2 0.7 all-gather.5.cloned.1.call-update
  7.9 6.1 convert_element_type.20
  14.0 0.0 reduce-scatter.5.cloned.1.call-start
  14.1 1.0 copy-done.3
  15.1 15.7 %all_gather.17 = bf16[256,1024]{1,0:T(8,128)(2,1)S(1)} all-gather(bf16[256,512]{1,0:T(8,128)(2,1)S(1)} %convert_element_type.22), channel_id=1, replica_groups=mesh['layer'=1,'col'=2,'row'=4] {'col'}, dimensions={1}, use_global_device_ids=true | all-gather | bytes 786432 | tf_op jit(solution)/shard_map/all_gather | solution.py:30
  30.8 39.7 %all-gather.5.cloned.1.call-done = f32[256,4096]{1,0:T(8,128)} async-done(((f32[256,2048]{1,0:T(8,128)}), f32[256,4096]{1,0:T(8,128)}) %all-gather.5.cloned.1.call-update) | async-done | bytes 4194320 | tf_op jit(solution)/shard_map/all_gather | solution.py:22
  70.5 107.5 %all-gather.7.cloned.1.call-done = bf16[4096,2048]{1,0:T(8,128)(2,1)} async-done(((bf16[1024,2048]{1,0:T(8,128)(2,1)}), bf16[4096,2048]{1,0:T(8,128)(2,1)}) %all-gather.7.cloned.1.call-update) | async-done | bytes 16777232 | tf_op jit(solution)/shard_map/all_gather | solution.py:31
  178.0 16.0 %convolution_bitcast_fusion = f32[1024,2048]{0,1:T(8,128)} fusion(bf16[256,1024]{1,0:T(8,128)(2,1)S(1)} %all_gather.17, bf16[4096,2048]{1,0:T(8,128)(2,1)} %all-gather.7.cloned.1.call-done, f32[256,4096]{1,0:T(8,128)} %all-gather.5.cloned.1.call-done), kind=kOutput, calls=%fused_computation.1 | convolution fusion | flops 5370281984 | bytes 29884416 | tf_op jit(solution)/shard_map/dot_general | solution.py:33
  194.1 0.0 all-gather.11.cloned.1.call-start
  194.1 0.5 all-gather.11.cloned.1.call-update
  194.7 1.0 copy-done.1
  195.7 1.8 copy.13
  197.5 2.9 copy.14
  200.4 59.0 %reduce-scatter.5.cloned.1.call-done = f32[256,2048]{0,1:T(8,128)} async-done(((f32[1024,2048]{0,1:T(8,128)}), f32[256,2048]{0,1:T(8,128)}) %reduce-scatter.5.cloned.1.call-update) | async-done | bytes 2097168 | tf_op jit(solution)/shard_map/reduce_scatter | solution.py:34
  259.3 6.4 divide_convert_fusion
  265.8 0.2 reduce-scatter.9.cloned.1.call-start
  266.0 50.5 %all-gather.11.cloned.1.call-done = f32[1024,2048]{1,0:T(8,128)} async-done(((f32[256,2048]{1,0:T(8,128)}), f32[1024,2048]{1,0:T(8,128)}) %all-gather.11.cloned.1.call-update) | async-done | bytes 8388624 | tf_op jit(solution)/shard_map/all_gather | solution.py:23
  316.5 10.4 %fusion.5 = f32[256,1024]{1,0:T(8,128)} fusion(f32[256,2048]{1,0:T(8,128)S(1)} %copy-done, f32[1024,2048]{1,0:T(8,128)} %all-gather.11.cloned.1.call-done), kind=kOutput, calls=%fused_computation.11 | convolution fusion | flops 6442450944 | bytes 11534336 | tf_op jit(solution)/shard_map/dot_general | solution.py:24
  326.9 0.0 reduce-scatter.7.cloned.1.call-start
  326.9 23.6 %all-gather.9.cloned.1.call-done = bf16[1024,2048]{0,1:T(8,128)(2,1)} async-done(((bf16[256,2048]{0,1:T(8,128)(2,1)}), bf16[1024,2048]{0,1:T(8,128)(2,1)}) %all-gather.9.cloned.1.call-update) | async-done | bytes 4194320 | tf_op jit(solution)/shard_map/all_gather | solution.py:38
  350.5 16.6 %fusion.7 = f32[256,4096]{0,1:T(8,128)} fusion(bf16[4096,2048]{1,0:T(8,128)(2,1)} %all-gather.7.cloned.1.call-done, bf16[1024,2048]{0,1:T(8,128)(2,1)} %all-gather.9.cloned.1.call-done, bf16[256,1024]{1,0:T(8,128)(2,1)S(1)} %all_gather.17), kind=kOutput, calls=%fused_computation.13 | convolution fusion | flops 5369233408 | bytes 25690112 | tf_op jit(solution)/shard_map/dot_general | solution.py:40
  367.2 0.3 reduce-scatter.11.cloned.1.call-start
  367.4 31.6 %fusion.6 = f32[4096,2048]{1,0:T(8,128)} fusion(f32[256,4096]{1,0:T(8,128)} %all-gather.5.cloned.1.call-done, f32[256,2048]{1,0:T(8,128)S(1)} %copy-done), kind=kOutput, calls=%fused_computation.12 | convolution fusion | flops 25769803776 | bytes 39845888 | tf_op jit(solution)/shard_map/dot_general | solution.py:26
  399.1 2.0 copy.16
  401.1 1.9 multiply_add_fusion.2
  403.1 2.9 copy.18
  405.9 2.9 copy.19
  408.8 16.2 %reduce-scatter.7.cloned.1.call-done = f32[256,2048]{0,1:T(8,128)} async-done(((f32[256,4096]{0,1:T(8,128)}), f32[256,2048]{0,1:T(8,128)}) %reduce-scatter.7.cloned.1.call-update) | async-done | bytes 2097168 | tf_op jit(solution)/shard_map/reduce_scatter | solution.py:41
  425.0 3.2 multiply_subtract_fusion
  428.2 2.9 copy.17
  431.1 222.5 %reduce-scatter.11.cloned.1.call-done = f32[1024,2048]{1,0:T(8,128)} async-done(((f32[4096,2048]{1,0:T(8,128)}), f32[1024,2048]{1,0:T(8,128)}) %reduce-scatter.11.cloned.1.call-update) | async-done | bytes 8388624 | tf_op jit(solution)/shard_map/reduce_scatter | solution.py:27
  653.6 12.1 %multiply_add_fusion = f32[1024,2048]{1,0:T(8,128)} fusion(f32[1024,2048]{1,0:T(8,128)} %reduce-scatter.11.cloned.1.call-done, f32[1024,2048]{1,0:T(8,128)} %param.13), kind=kLoop, calls=%fused_computation | loop fusion | flops 6291456 | bytes 25165824 | tf_op jit(solution)/shard_map/add | solution.py:29
  (17 shorter events, 0.3 us)
Async XLA Ops:
  7.2 63.3 %all-gather.5.cloned.1.call-start = ((), (), s32[]{:S(2)}) async-start(), calls=%async_computation.4 | async-start | bytes 6291456 | tf_op jit(solution)/shard_map/all_gather | solution.py:22
  7.9 170.1 %all-gather.7.cloned.1.call-start = ((), (), s32[]{:S(2)}) async-start(), calls=%async_computation.5 | async-start | bytes 20971520 | tf_op jit(solution)/shard_map/all_gather | solution.py:31
  14.0 1.0 copy-start.3
  14.0 245.3 %reduce-scatter.5.cloned.1.call-start = ((), (), s32[]{:S(2)}) async-start(), calls=%async_computation.6 | async-start | bytes 10485760 | tf_op jit(solution)/shard_map/reduce_scatter | solution.py:34
  194.1 1.6 copy-start.1
  194.1 122.4 %all-gather.11.cloned.1.call-start = ((), (), s32[]{:S(2)}) async-start(), calls=%async_computation.9 | async-start | bytes 10485760 | tf_op jit(solution)/shard_map/all_gather | solution.py:23
  194.7 155.8 %all-gather.9.cloned.1.call-start = ((), (), s32[]{:S(2)}) async-start(), calls=%async_computation.7 | async-start | bytes 5242880 | tf_op jit(solution)/shard_map/all_gather | solution.py:38
  259.3 57.1 %copy-start = (f32[256,2048]{1,0:T(8,128)S(1)}, f32[256,2048]{1,0:T(8,128)}, u32[]{:S(2)}) copy-start(f32[256,2048]{1,0:T(8,128)} %param.9) | copy-start | bytes 6291460
  265.8 135.3 %reduce-scatter.9.cloned.1.call-start = ((), (), s32[]{:S(2)}) async-start(), calls=%async_computation.10 | async-start | bytes 1572864 | tf_op jit(solution)/shard_map/reduce_scatter | solution.py:25
  326.9 98.2 %reduce-scatter.7.cloned.1.call-start = ((), (), s32[]{:S(2)}) async-start(), calls=%async_computation.8 | async-start | bytes 6291456 | tf_op jit(solution)/shard_map/reduce_scatter | solution.py:41
  367.2 286.5 %reduce-scatter.11.cloned.1.call-start = ((), (), s32[]{:S(2)}) async-start(), calls=%async_computation.11 | async-start | bytes 41943040 | tf_op jit(solution)/shard_map/reduce_scatter | solution.py:27
  399.1 2.0 copy-start.2
Sparse Core Ops, SparseCore 0:
  9.5 60.9 all-gather.4
  72.6 105.3 all-gather.6
  194.2 65.0 reduce-scatter.4
  260.7 55.7 all-gather.10
  318.4 32.0 all-gather.8
  353.1 17.5 reduce-scatter.8
  373.5 51.4 reduce-scatter.6
  427.6 226.0 reduce-scatter.10
where the time goes:
time: 673 us
  waiting for transfers between devices  520 us (77%)
  matrix products  74.7 us (11%)
  other arithmetic  29.7 us (4%)
  local copies, waits for them, and re-layouts  17.2 us (3%)
  blocking collectives  15.7 us (2%)
  between operations  14.2 us (2%)
    reduce_scatter x1, waiting for transfers between devices, local_step(): lax.psum_scatter(right_part, 'row', scatter_dimension=0, tiled=True)  223 us
    all_gather x1, waiting for transfers between devices, local_step(): lax.all_gather(basis_right.astype(jnp.bfloat16), 'row', axis=0, tiled=True)  108 us
    reduce_scatter x1, waiting for transfers between devices, local_step(): lax.psum_scatter(rotated_part, 'row', scatter_dimension=0, tiled=True)  59 us
    all_gather x1, waiting for transfers between devices, local_step(): grad_cols = lax.all_gather(grad_in, 'row', axis=0, tiled=True)  50.5 us
    all_gather x1, waiting for transfers between devices, local_step(): grad_rows = lax.all_gather(grad_in, 'col', axis=1, tiled=True)  39.7 us
    dot_general x1, matrix products, local_step(): lax.dot_general(grad_rows, grad_in, contract_rows, precision=highest, pre...  31.6 us
    all_gather x1, waiting for transfers between devices, local_step(): lax.all_gather(direction.astype(jnp.bfloat16), 'row', axis=0, tiled=True)  23.6 us
    unnamed x14, local copies, waits for them, and re-layouts  17.2 us
  transfers between devices with their start and end apart: 8, of which 7 were waited for; matrix products, arithmetic and copies ran while one was open for 14% of the time, Pallas kernels for 0%

commit v1 on v0

v1 whole, which is shorter than its diff:
```python
import jax
import jax.numpy as jnp
from jax import lax
from jax.sharding import PartitionSpec as P

BETA1 = 0.9
BETA2 = 0.9
EPS = 1e-8
LR = 0.1
STEP = 10
BIAS_ONE = 1.0 - BETA1 ** STEP
BIAS_TWO = 1.0 - BETA2 ** STEP


def _pairs(move, keep=None):
    pairs = []
    for y in range(2):
        for x in range(2):
            for c in range(2):
                if keep is None or keep(y, x):
                    ny, nx, nc = move(y, x, c)
                    pairs.append((4 * y + 2 * x + c, 4 * ny + 2 * nx + nc))
    return pairs


PAIRS_X = _pairs(lambda y, x, c: (y, 1 - x, c))
PAIRS_Y = _pairs(lambda y, x, c: (1 - y, x, c))
PAIRS_CORE = _pairs(lambda y, x, c: (y, x, 1 - c))
PAIRS_Y_DIAG_OFF = _pairs(lambda y, x, c: (1 - y, x, c), lambda y, x: x == y)
PAIRS_Y_OFF_DIAG = _pairs(lambda y, x, c: (1 - y, x, c), lambda y, x: x != y)
PAIRS_X_DIAG_OFF = _pairs(lambda y, x, c: (y, 1 - x, c), lambda y, x: x == y)
PAIRS_CROSS = _pairs(lambda y, x, c: (1 - y, 1 - x, c), lambda y, x: x != y)


def _send(value, pairs):
    return lax.ppermute(value, ("col", "row"), pairs)


def solution(mesh):
    tile_spec = P(("layer", "row"), "col")
    highest = lax.Precision.HIGHEST
    contract_rows = (((0,), (0,)), ((), ()))
    contract_cols = (((1,), (1,)), ((), ()))
    f32, bf16 = jnp.float32, jnp.bfloat16

    def local_step(weight, grad_in, mom_first, mom_second, stat_left, stat_right, basis_left, basis_right):
        y, r = lax.axis_index("col"), lax.axis_index("row")
        x, c = r // 2, r % 2
        on_diag = x == y
        half = grad_in.shape[1] // 2
        rows = grad_in.shape[0]

        def mine(array):
            return lax.dynamic_slice_in_dim(array, c * half, half, 1)

        def theirs(array):
            return lax.dynamic_slice_in_dim(array, (1 - c) * half, half, 1)

        def place(own, other):
            return jnp.where(c == 0, jnp.concatenate([own, other], 1), jnp.concatenate([other, own], 1))

        g0 = grad_in
        g2 = _send(g0, PAIRS_X)
        g1 = _send(g0, PAIRS_CORE)
        g3 = _send(g2, PAIRS_CORE)
        pieces = [g0, g1, g2, g3]
        left = [jnp.where(on_diag, mine(p), _send(mine(p), PAIRS_Y_DIAG_OFF)) for p in pieces]
        left_bf = [p.astype(bf16) for p in left]
        part_bf = [_send(p, PAIRS_CORE) for p in left_bf]
        part_bf = [part_bf[1], part_bf[0], part_bf[3], part_bf[2]]

        right_bf = basis_right.astype(bf16)
        right_mine, right_theirs = mine(right_bf), theirs(right_bf)
        right_part = _send(right_theirs, PAIRS_CORE)

        q0 = basis_left.astype(bf16)
        q2 = _send(q0, PAIRS_X)
        qa = jnp.concatenate([q0, q2], 0)
        qb = _send(qa, PAIRS_Y)
        qm = jnp.stack([jnp.where(on_diag, qa, qb), jnp.where(on_diag, qb, qa)])
        qp = _send(qm, PAIRS_CORE)
        cols = []
        for k in range(2):
            block = jnp.concatenate([qm[k, :rows], qp[k, :rows], qm[k, rows:], qp[k, rows:]], 0)
            swapped = jnp.concatenate([block[:, rows:], block[:, :rows]], 1)
            cols.append(jnp.where(c == 0, block, swapped))
        left_all = jnp.concatenate(cols, 1)

        def inner(k):
            a = jnp.concatenate([left_bf[k], left_bf[k + 1]], 0)
            b = jnp.concatenate([part_bf[k], part_bf[k + 1]], 0)
            return jnp.dot(a, right_mine, preferred_element_type=f32) + jnp.dot(b, right_part, preferred_element_type=f32)

        far = _send(inner(2), PAIRS_X)
        h_own = (inner(0) + far).astype(bf16)
        h_far = _send(h_own, PAIRS_X)
        h_all = jnp.concatenate([h_own, h_far], 0)
        rotated = lax.dot_general(left_all[:, : 2 * rows], h_all, contract_rows, preferred_element_type=f32)

        first = jnp.concatenate([mine(mom_first), _send(theirs(mom_first), PAIRS_CORE)], 0)
        second = jnp.concatenate([mine(mom_second), _send(theirs(mom_second), PAIRS_CORE)], 0)
        new_first = BETA1 * first + (1.0 - BETA1) * rotated
        new_second = BETA2 * second + (1.0 - BETA2) * rotated * rotated
        direction = ((new_first / BIAS_ONE) / (jnp.sqrt(new_second / BIAS_TWO) + EPS)).astype(bf16)
        dir_all = jnp.concatenate([direction, _send(direction, PAIRS_X)], 0)
        back = jnp.dot(left_all, dir_all, preferred_element_type=f32).astype(bf16)
        back_p = _send(back, PAIRS_CORE)
        back_p = jnp.concatenate([back_p[rows : 2 * rows], back_p[:rows], back_p[3 * rows :], back_p[2 * rows : 3 * rows]], 0)

        def update(lo):
            a, b = back[lo : lo + 2 * rows], back_p[lo : lo + 2 * rows]
            return lax.dot_general(a, right_mine, contract_cols, preferred_element_type=f32) + lax.dot_general(
                b, right_theirs, contract_cols, preferred_element_type=f32
            )

        up_far = update(2 * rows)
        up_near = update(0)
        total = (
            jnp.where(on_diag, up_near, 0.0)
            + _send(up_near, PAIRS_Y_OFF_DIAG)
            + _send(up_far, PAIRS_X_DIAG_OFF)
            + _send(up_far, PAIRS_CROSS)
        )
        new_weight = weight - LR * place(total[:rows], _send(total[rows:], PAIRS_CORE))
        out_first = place(new_first[:rows], _send(new_first[rows:], PAIRS_CORE))
        out_second = place(new_second[:rows], _send(new_second[rows:], PAIRS_CORE))

        stat = [lax.dot_general(p, g0, contract_cols, precision=highest, preferred_element_type=f32).T for p in pieces]
        near = place(stat[0], stat[1])
        away = place(stat[2], stat[3])
        got = _send(jnp.where(on_diag, away, near), PAIRS_Y)
        new_left = BETA2 * stat_left + (1.0 - BETA2) * (jnp.where(on_diag, near, away) + got)
        wide = jnp.concatenate(pieces, 0)
        tall = jnp.concatenate(left, 0)
        right_sum = lax.dot_general(tall, wide, contract_rows, precision=highest, preferred_element_type=f32)
        new_right = BETA2 * stat_right + (1.0 - BETA2) * right_sum
        return new_weight, out_first, out_second, new_left, new_right

    return jax.shard_map(local_step, mesh=mesh, in_specs=(tile_spec,) * 8, out_specs=(tile_spec,) * 5, check_vma=False)
```

time: 673 us -> 390 us (0.58)
  waiting for transfers between devices: 520 us -> 232 us
  starting transfers between devices: 0.72 us -> 35.1 us
  blocking collectives: 15.7 us -> 0 us
  between operations: 14.2 us -> 1.02 us
    reduce_scatter x4 -> x0, waiting for transfers between devices: 298 us -> none  [the longest x1 223 us: local_step(): lax.psum_scatter(right_part, 'row', scatter_dimension=0, tiled=True)]
    ppermute x0 -> x28, waiting for transfers between devices: none -> 232 us  [_send(): return lax.ppermute(value, ('col', 'row'), pairs)]
    all_gather x4 -> x0, waiting for transfers between devices: 221 us -> none  [the longest x1 108 us: local_step(): lax.all_gather(basis_right.astype(jnp.bfloat16), 'row', axis=0, tiled=True)]
    ppermute x0 -> x28, starting transfers between devices: none -> 35.1 us  [_send(): return lax.ppermute(value, ('col', 'row'), pairs)]
    all_gather x1 -> x0, blocking collectives: 15.7 us -> none  [local_step(): lax.all_gather(basis_left.astype(jnp.bfloat16), 'col', axis=1, tiled=True)]
    unnamed x14 -> x32, local copies, waits for them, and re-layouts: 17.2 us -> 6.75 us
    dynamic_slice x0 -> x7, local copies, waits for them, and re-layouts: none -> 10.1 us  [the longest x6 7.07 us: mine(): return lax.dynamic_slice_in_dim(array, c * half, half, 1)]
    add x2, other arithmetic: 14.1 us -> 6.72 us  [the longest x1 4.57 us: local_step(): jnp.where(on_diag, up_near, 0.0) + _send(up_near, PAIRS_Y_OFF_DIAG)]
  transfers between devices with their start and end apart: 8 -> 28, of which waited for: 7 -> 8; matrix products, arithmetic and copies ran while one was open for 14% -> 27% of each run, Pallas kernels for 0% -> 0%
where the time goes in v1:
time: 390 us; the launch traced here: 389 us
  waiting for transfers between devices  232 us (59%)
  matrix products  71.6 us (18%)
  starting transfers between devices  35.1 us (9%)
  other arithmetic  29.4 us (8%)
  local copies, waits for them, and re-layouts  19.5 us (5%)
    ppermute x28, waiting for transfers between devices, _send(): return lax.ppermute(value, ('col', 'row'), pairs)  232 us
    ppermute x28, starting transfers between devices, _send(): return lax.ppermute(value, ('col', 'row'), pairs)  35.1 us
    dot_general x1, matrix products, local_step(): lax.dot_general(tall, wide, contract_rows, precision=highest, preferred_e...  31 us
    dot_general x4, matrix products, local_step(): lax.dot_general(p, g0, contract_cols, precision=highest, preferred_elemen...  10.6 us
    dot_general x2, matrix products, update(): lax.dot_general(b, right_theirs, contract_cols, preferred_element_type=f32)  8.59 us
  transfers between devices with their start and end apart: 28, of which 8 were waited for; matrix products, arithmetic and copies ran while one was open for 27% of the time, Pallas kernels for 0%

profile of v1, /device:TPU:0, one launch (start us, length us, event | category | flops | bytes accessed | tf_op | source)
XLA Modules:
  0.0 388.8 jit_solution(4304289203712489511)
XLA Ops:
  0.6 3.4 collective-permute-start.10
  4.0 45.6 %collective-permute-done.10 = f32[256,2048]{1,0:T(8,128)S(1)} collective-permute-done((f32[256,2048]{1,0:T(8,128)}, f32[256,2048]{1,0:T(8,128)S(1)}, u32[]{:S(2)}, u32[]{:S(2)}) %collective-permute-start.10) | collective-permute-done | bytes 2097184 | tf_op jit(solution)/shard_map/ppermute | solution.py:36
  50.1 6.3 %convert_element_type.30 = bf16[1024,2048]{1,0:T(8,128)(2,1)} convert(f32[1024,2048]{1,0:T(8,128)} %param.15) | non-fusion elementwise | flops 2097152 | bytes 12582912 | tf_op jit(solution)/shard_map/convert_element_type | solution.py:72
  56.5 4.7 %collective-permute-start.11 = (f32[256,1024]{1,0:T(8,128)S(1)}, f32[256,1024]{1,0:T(8,128)}, u32[]{:S(2)}, u32[]{:S(2)}) collective-permute-start(f32[256,1024]{1,0:T(8,128)S(1)} %constant_dynamic-slice_fusion.3), channel_id=1, source_target_pairs={{0,4},{1,5},{6,2},{7,3}} | collective-permute-start | bytes 3145736 | tf_op jit(solution)/shard_map/ppermute | solution.py:36
  61.1 3.1 constant_dynamic-slice_fusion.4
  64.2 2.3 constant_dynamic-slice_fusion.2
  68.8 14.9 %collective-permute-done.11 = f32[256,1024]{1,0:T(8,128)} collective-permute-done((f32[256,1024]{1,0:T(8,128)S(1)}, f32[256,1024]{1,0:T(8,128)}, u32[]{:S(2)}, u32[]{:S(2)}) %collective-permute-start.11) | collective-permute-done | bytes 1048608 | tf_op jit(solution)/shard_map/ppermute | solution.py:36
  84.9 20.0 %collective-permute-done.13 = f32[256,1024]{1,0:T(8,128)} collective-permute-done((f32[256,1024]{1,0:T(8,128)}, f32[256,1024]{1,0:T(8,128)}, u32[]{:S(2)}, u32[]{:S(2)}) %collective-permute-start.13) | collective-permute-done | bytes 1048608 | tf_op jit(solution)/shard_map/ppermute | solution.py:36
  105.0 2.4 fusion.81
  108.5 5.7 %collective-permute-start.4 = (f32[256,1024]{1,0:T(8,128)}, f32[256,1024]{1,0:T(8,128)}, u32[]{:S(2)}, u32[]{:S(2)}) collective-permute-start(f32[256,1024]{1,0:T(8,128)} %constant_dynamic-slice_fusion.6), channel_id=1, source_target_pairs={{0,4},{1,5},{6,2},{7,3}} | collective-permute-start | bytes 3145736 | tf_op jit(solution)/shard_map/ppermute | solution.py:36
  114.2 2.3 constant_dynamic-slice_fusion.5
  116.5 2.6 collective-permute-start.6
  119.1 2.8 fusion.54
  122.0 2.6 convolution_add_fusion.2
  127.8 50.2 %collective-permute-done = bf16[256,512]{1,0:T(8,128)(2,1)} collective-permute-done((bf16[256,512]{1,0:T(8,128)(2,1)S(1)}, bf16[256,512]{1,0:T(8,128)(2,1)}, u32[]{:S(2)}, u32[]{:S(2)}) %collective-permute-start) | collective-permute-done | bytes 262176 | tf_op jit(solution)/shard_map/ppermute | solution.py:36
  180.5 2.6 fusion.79
  183.6 8.7 %collective-permute-done.1 = bf16[512,512]{1,0:T(8,128)(2,1)S(1)} collective-permute-done((bf16[512,512]{1,0:T(8,128)(2,1)S(1)}, bf16[512,512]{1,0:T(8,128)(2,1)S(1)}, u32[]{:S(2)}, u32[]{:S(2)}) %collective-permute-start.1) | collective-permute-done | bytes 524320 | tf_op jit(solution)/shard_map/ppermute | solution.py:36
  194.1 3.1 fusion.47
  197.3 2.9 add_convert_fusion
  201.4 23.8 %collective-permute-done.17 = bf16[512,1024]{1,0:T(8,128)(2,1)S(1)} collective-permute-done((bf16[512,1024]{1,0:T(8,128)(2,1)S(1)}, bf16[512,1024]{1,0:T(8,128)(2,1)S(1)}, u32[]{:S(2)}, u32[]{:S(2)}) %collective-permute-start.17) | collective-permute-done | bytes 1048608 | tf_op jit(solution)/shard_map/ppermute | solution.py:36
  225.1 5.0 %divide_convert_fusion = (bf16[512,1024]{1,0:T(8,128)(2,1)S(1)}, f32[512,1024]{1,0:T(8,128)}, f32[512,1024]{1,0:T(8,128)}) fusion(f32[256,1024]{1,0:T(8,128)S(1)} %collective-permute-done.3, f32[256,1024]{1,0:T(8,128)S(1)} %get-tuple-element.33, f32[256,1024]{1,0:T(8,128)} %collective-permute-done.18, f32[256,1024]{1,0:T(8,128)S(1)} %get-tuple-element.31, ...), kind=kOutput, calls=%fused_computation.38 | convolution fusion | flops 1084751872 | bytes 12582912 | tf_op jit(solution)/shard_map/dot_general | solution.py:98
  231.1 23.1 %collective-permute-done.19 = bf16[512,1024]{1,0:T(8,128)(2,1)S(1)} collective-permute-done((bf16[512,1024]{1,0:T(8,128)(2,1)S(1)}, bf16[512,1024]{1,0:T(8,128)(2,1)S(1)}, u32[]{:S(2)}, u32[]{:S(2)}) %collective-permute-start.19) | collective-permute-done | bytes 1048608 | tf_op jit(solution)/shard_map/ppermute | solution.py:36
  254.2 2.3 fusion.31
  263.1 4.2 %convolution_add_fusion = f32[512,1024]{1,0:T(8,128)} fusion(f32[512,1024]{1,0:T(8,128)S(1)} %fusion.36, bf16[1024,1024]{1,0:T(8,128)(2,1)} %constant_dynamic-slice_fusion.4, bf16[256,1024]{1,0:T(8,128)(2,1)S(1)} %get-tuple-element.28, bf16[256,1024]{1,0:T(8,128)(2,1)S(1)} %get-tuple-element.29), kind=kOutput, calls=%fused_computation.41 | convolution fusion | flops 1076363264 | bytes 7340032 | tf_op jit(solution)/shard_map/dot_general | solution.py:112
  267.4 3.8 collective-permute-start.22
  273.2 4.3 %convolution_add_fusion.1 = f32[512,1024]{1,0:T(8,128)} fusion(f32[512,1024]{1,0:T(8,128)S(1)} %fusion.38, bf16[1024,1024]{1,0:T(8,128)(2,1)} %constant_dynamic-slice_fusion.4, bf16[256,1024]{1,0:T(8,128)(2,1)S(1)} %get-tuple-element.30, bf16[256,1024]{1,0:T(8,128)(2,1)S(1)} %get-tuple-element.27), kind=kOutput, calls=%fused_computation.42 | convolution fusion | flops 1076363264 | bytes 7340032 | tf_op jit(solution)/shard_map/dot_general | solution.py:112
  279.1 3.5 fusion.90
  282.5 3.4 fusion.92
  286.8 3.7 collective-permute-start.27
  292.6 45.8 %collective-permute-done.27 = f32[256,512]{0,1:T(8,128)} collective-permute-done((f32[256,512]{0,1:T(8,128)}, f32[256,512]{0,1:T(8,128)}, u32[]{:S(2)}, u32[]{:S(2)}) %collective-permute-start.27) | collective-permute-done | bytes 524320 | tf_op jit(solution)/shard_map/ppermute | solution.py:36
  345.2 4.6 %add_add_fusion = f32[512,1024]{1,0:T(8,128)S(1)} fusion(f32[512,1024]{1,0:T(8,128)} %collective-permute-done.23, f32[512,1024]{1,0:T(8,128)} %collective-permute-done.22, f32[512,1024]{1,0:T(8,128)} %collective-permute-done.21, f32[512,1024]{1,0:T(8,128)} %convolution_add_fusion.1, pred[]{:T(512)S(6)} %eq.7), kind=kLoop, calls=%fused_computation.37 | loop fusion | flops 2097152 | bytes 10485761 | tf_op jit(solution)/shard_map/add | solution.py:119
  351.9 31.0 %multiply_add_fusion = f32[1024,2048]{1,0:T(8,128)} fusion(f32[1024,2048]{1,0:T(8,128)} %param.13, f32[256,2048]{1,0:T(8,128)} %collective-permute-done.12, f32[256,2048]{1,0:T(8,128)S(1)} %copy-done.5, f32[256,2048]{1,0:T(8,128)} %collective-permute-done.5, f32[256,2048]{1,0:T(8,128)S(1)} %copy-done, f32[256,1024]{1,0:T(8,128)S(1)} %copy-done.11, ...), kind=kOutput, calls=%fused_computation.8 | convolution fusion | flops 25785532416 | bytes 29360128 | tf_op jit(solution)/shard_map/dot_general | solution.py:135
  (105 shorter events, 43.1 us)
Async XLA Ops:
  0.6 49.0 %collective-permute-start.10 = (f32[256,2048]{1,0:T(8,128)}, f32[256,2048]{1,0:T(8,128)S(1)}, u32[]{:S(2)}, u32[]{:S(2)}) collective-permute-start(f32[256,2048]{1,0:T(8,128)} %param.9), channel_id=1, source_target_pairs={{0,2},{1,3},{2,0},{3,1},{4,6},{5,7},{6,4},{7,5}} | collective-permute-start | bytes 6291464 | tf_op jit(solution)/shard_map/ppermute | solution.py:36
  49.6 34.0 %copy-start.3 = (f32[256,2048]{1,0:T(8,128)}, f32[256,2048]{1,0:T(8,128)S(1)}, u32[]{:S(2)}) copy-start(f32[256,2048]{1,0:T(8,128)S(1)} %collective-permute-done.10) | copy-start | bytes 6291460
  49.6 14.6 %collective-permute-start.12 = (f32[256,2048]{1,0:T(8,128)S(1)}, f32[256,2048]{1,0:T(8,128)}, u32[]{:S(2)}, u32[]{:S(2)}) collective-permute-start(f32[256,2048]{1,0:T(8,128)S(1)} %collective-permute-done.10), channel_id=1, source_target_pairs={{0,1},{1,0},{2,3},{3,2},{4,5},{5,4},{6,7},{7,6}} | collective-permute-start | bytes 6291464 | tf_op jit(solution)/shard_map/ppermute | solution.py:36
  49.6 64.6 %collective-permute-start.5 = (f32[256,2048]{1,0:T(8,128)}, f32[256,2048]{1,0:T(8,128)}, u32[]{:S(2)}, u32[]{:S(2)}) collective-permute-start(f32[256,2048]{1,0:T(8,128)} %param.9), channel_id=1, source_target_pairs={{0,1},{1,0},{2,3},{3,2},{4,5},{5,4},{6,7},{7,6}} | collective-permute-start | bytes 6291464 | tf_op jit(solution)/shard_map/ppermute | solution.py:36
  56.5 27.2 %collective-permute-start.11 = (f32[256,1024]{1,0:T(8,128)S(1)}, f32[256,1024]{1,0:T(8,128)}, u32[]{:S(2)}, u32[]{:S(2)}) collective-permute-start(f32[256,1024]{1,0:T(8,128)S(1)} %constant_dynamic-slice_fusion.3), channel_id=1, source_target_pairs={{0,4},{1,5},{6,2},{7,3}} | collective-permute-start | bytes 3145736 | tf_op jit(solution)/shard_map/ppermute | solution.py:36
  64.2 54.9 %collective-permute-start.9 = (bf16[1024,1024]{1,0:T(8,128)(2,1)}, bf16[1024,1024]{1,0:T(8,128)(2,1)}, u32[]{:S(2)}, u32[]{:S(2)}) collective-permute-start(bf16[1024,1024]{1,0:T(8,128)(2,1)} %constant_dynamic-slice_fusion.4), channel_id=1, source_target_pairs={{0,1},{1,0},{2,3},{3,2},{4,5},{5,4},{6,7},{7,6}} | collective-permute-start | bytes 6291464 | tf_op jit(solution)/shard_map/ppermute | solution.py:36
  66.5 38.4 %collective-permute-start.13 = (f32[256,1024]{1,0:T(8,128)}, f32[256,1024]{1,0:T(8,128)}, u32[]{:S(2)}, u32[]{:S(2)}) collective-permute-start(f32[256,1024]{1,0:T(8,128)} %constant_dynamic-slice_fusion.2), channel_id=1, source_target_pairs={{0,4},{1,5},{6,2},{7,3}} | collective-permute-start | bytes 3145736 | tf_op jit(solution)/shard_map/ppermute | solution.py:36
  84.9 22.5 %copy-start = (f32[256,2048]{1,0:T(8,128)S(1)}, f32[256,2048]{1,0:T(8,128)}, u32[]{:S(2)}) copy-start(f32[256,2048]{1,0:T(8,128)} %param.9) | copy-start | bytes 6291460
  84.9 34.2 %collective-permute-start.15 = (bf16[256,1024]{1,0:T(8,128)(2,1)S(1)}, bf16[256,1024]{1,0:T(8,128)(2,1)S(1)}, u32[]{:S(2)}, u32[]{:S(2)}) collective-permute-start(bf16[256,1024]{1,0:T(8,128)(2,1)S(1)} %get-tuple-element.19), channel_id=1, source_target_pairs={{0,1},{1,0},{2,3},{3,2},{4,5},{5,4},{6,7},{7,6}} | collective-permute-start | bytes 1572872 | tf_op jit(solution)/shard_map/ppermute | solution.py:36
  107.4 11.8 %collective-permute-start.14 = (bf16[256,1024]{1,0:T(8,128)(2,1)S(1)}, bf16[256,1024]{1,0:T(8,128)(2,1)S(1)}, u32[]{:S(2)}, u32[]{:S(2)}) collective-permute-start(bf16[256,1024]{1,0:T(8,128)(2,1)S(1)} %get-tuple-element.17), channel_id=1, source_target_pairs={{0,1},{1,0},{2,3},{3,2},{4,5},{5,4},{6,7},{7,6}} | collective-permute-start | bytes 1572872 | tf_op jit(solution)/shard_map/ppermute | solution.py:36
  108.5 70.7 %collective-permute-start.4 = (f32[256,1024]{1,0:T(8,128)}, f32[256,1024]{1,0:T(8,128)}, u32[]{:S(2)}, u32[]{:S(2)}) collective-permute-start(f32[256,1024]{1,0:T(8,128)} %constant_dynamic-slice_fusion.6), channel_id=1, source_target_pairs={{0,4},{1,5},{6,2},{7,3}} | collective-permute-start | bytes 3145736 | tf_op jit(solution)/shard_map/ppermute | solution.py:36
  116.5 5.5 %copy-start.1 = (bf16[1024,2048]{1,0:T(8,128)(2,1)S(1)}, bf16[1024,2048]{1,0:T(8,128)(2,1)}, u32[]{:S(2)}) copy-start(bf16[1024,2048]{1,0:T(8,128)(2,1)} %convert_element_type.30) | copy-start | bytes 12582916
  116.5 64.0 %collective-permute-start.6 = (f32[256,1024]{1,0:T(8,128)}, f32[256,1024]{1,0:T(8,128)}, u32[]{:S(2)}, u32[]{:S(2)}) collective-permute-start(f32[256,1024]{1,0:T(8,128)} %constant_dynamic-slice_fusion.5), channel_id=1, source_target_pairs={{0,4},{1,5},{6,2},{7,3}} | collective-permute-start | bytes 3145736 | tf_op jit(solution)/shard_map/ppermute | solution.py:36
  124.6 72.6 %collective-permute-start.16 = (f32[512,1024]{1,0:T(8,128)}, f32[512,1024]{1,0:T(8,128)}, u32[]{:S(2)}, u32[]{:S(2)}) collective-permute-start(f32[512,1024]{1,0:T(8,128)} %convolution_add_fusion.2), channel_id=1, source_target_pairs={{0,2},{1,3},{2,0},{3,1},{4,6},{5,7},{6,4},{7,5}} | collective-permute-start | bytes 6291464 | tf_op jit(solution)/shard_map/ppermute | solution.py:36
  124.7 53.3 %collective-permute-start = (bf16[256,512]{1,0:T(8,128)(2,1)S(1)}, bf16[256,512]{1,0:T(8,128)(2,1)}, u32[]{:S(2)}, u32[]{:S(2)}) collective-permute-start(bf16[256,512]{1,0:T(8,128)(2,1)S(1)} %convert_element_type.27), channel_id=1, source_target_pairs={{0,2},{1,3},{2,0},{3,1},{4,6},{5,7},{6,4},{7,5}} | collective-permute-start | bytes 786440 | tf_op jit(solution)/shard_map/ppermute | solution.py:36
  127.8 73.5 %collective-permute-start.18 = (f32[256,1024]{1,0:T(8,128)}, f32[256,1024]{1,0:T(8,128)}, u32[]{:S(2)}, u32[]{:S(2)}) collective-permute-start(f32[256,1024]{1,0:T(8,128)} %get-tuple-element.32), channel_id=1, source_target_pairs={{0,1},{1,0},{2,3},{3,2},{4,5},{5,4},{6,7},{7,6}} | collective-permute-start | bytes 3145736 | tf_op jit(solution)/shard_map/ppermute | solution.py:36
  179.0 13.3 %collective-permute-start.1 = (bf16[512,512]{1,0:T(8,128)(2,1)S(1)}, bf16[512,512]{1,0:T(8,128)(2,1)S(1)}, u32[]{:S(2)}, u32[]{:S(2)}) collective-permute-start(bf16[512,512]{1,0:T(8,128)(2,1)S(1)} %pad_maximum_fusion.3), channel_id=1, source_target_pairs={{0,4},{1,5},{2,6},{3,7},{4,0},{5,1},{6,2},{7,3}} | collective-permute-start | bytes 1572872 | tf_op jit(solution)/shard_map/ppermute | solution.py:36
  180.5 13.1 %collective-permute-start.8 = (bf16[256,1024]{1,0:T(8,128)(2,1)S(1)}, bf16[256,1024]{1,0:T(8,128)(2,1)S(1)}, u32[]{:S(2)}, u32[]{:S(2)}) collective-permute-start(bf16[256,1024]{1,0:T(8,128)(2,1)S(1)} %get-tuple-element.15), channel_id=1, source_target_pairs={{0,1},{1,0},{2,3},{3,2},{4,5},{5,4},{6,7},{7,6}} | collective-permute-start | bytes 1572872 | tf_op jit(solution)/shard_map/ppermute | solution.py:36
  183.1 11.0 %collective-permute-start.7 = (bf16[256,1024]{1,0:T(8,128)(2,1)S(1)}, bf16[256,1024]{1,0:T(8,128)(2,1)S(1)}, u32[]{:S(2)}, u32[]{:S(2)}) collective-permute-start(bf16[256,1024]{1,0:T(8,128)(2,1)S(1)} %get-tuple-element.13), channel_id=1, source_target_pairs={{0,1},{1,0},{2,3},{3,2},{4,5},{5,4},{6,7},{7,6}} | collective-permute-start | bytes 1572872 | tf_op jit(solution)/shard_map/ppermute | solution.py:36
  192.3 9.0 %collective-permute-start.3 = (f32[256,1024]{1,0:T(8,128)S(1)}, f32[256,1024]{1,0:T(8,128)S(1)}, u32[]{:S(2)}, u32[]{:S(2)}) collective-permute-start(f32[256,1024]{1,0:T(8,128)S(1)} %get-tuple-element.34), channel_id=1, source_target_pairs={{0,1},{1,0},{2,3},{3,2},{4,5},{5,4},{6,7},{7,6}} | collective-permute-start | bytes 3145736 | tf_op jit(solution)/shard_map/ppermute | solution.py:36
  193.6 7.2 %collective-permute-start.2 = (bf16[2,512,512]{2,1,0:T(8,128)(2,1)S(1)}, bf16[2,512,512]{2,1,0:T(8,128)(2,1)S(1)}, u32[]{:S(2)}, u32[]{:S(2)}) collective-permute-start(bf16[2,512,512]{2,1,0:T(8,128)(2,1)S(1)} %pad_maximum_fusion), channel_id=1, source_target_pairs={{0,1},{1,0},{2,3},{3,2},{4,5},{5,4},{6,7},{7,6}} | collective-permute-start | bytes 3145736 | tf_op jit(solution)/shard_map/ppermute | solution.py:36
  200.2 25.0 %collective-permute-start.17 = (bf16[512,1024]{1,0:T(8,128)(2,1)S(1)}, bf16[512,1024]{1,0:T(8,128)(2,1)S(1)}, u32[]{:S(2)}, u32[]{:S(2)}) collective-permute-start(bf16[512,1024]{1,0:T(8,128)(2,1)S(1)} %add_convert_fusion), channel_id=1, source_target_pairs={{0,2},{1,3},{2,0},{3,1},{4,6},{5,7},{6,4},{7,5}} | collective-permute-start | bytes 3145736 | tf_op jit(solution)/shard_map/ppermute | solution.py:36
  230.1 24.1 %collective-permute-start.19 = (bf16[512,1024]{1,0:T(8,128)(2,1)S(1)}, bf16[512,1024]{1,0:T(8,128)(2,1)S(1)}, u32[]{:S(2)}, u32[]{:S(2)}) collective-permute-start(bf16[512,1024]{1,0:T(8,128)(2,1)S(1)} %get-tuple-element.10), channel_id=1, source_target_pairs={{0,2},{1,3},{2,0},{3,1},{4,6},{5,7},{6,4},{7,5}} | collective-permute-start | bytes 3145736 | tf_op jit(solution)/shard_map/ppermute | solution.py:36
  256.5 6.4 %collective-permute-start.20 = (bf16[1024,1024]{1,0:T(8,128)(2,1)S(1)}, bf16[1024,1024]{1,0:T(8,128)(2,1)S(1)}, u32[]{:S(2)}, u32[]{:S(2)}) collective-permute-start(bf16[1024,1024]{1,0:T(8,128)(2,1)S(1)} %fusion.31), channel_id=1, source_target_pairs={{0,1},{1,0},{2,3},{3,2},{4,5},{5,4},{6,7},{7,6}} | collective-permute-start | bytes 6291464 | tf_op jit(solution)/shard_map/ppermute | solution.py:36
  267.4 77.8 %collective-permute-start.22 = (f32[512,1024]{1,0:T(8,128)}, f32[512,1024]{1,0:T(8,128)}, u32[]{:S(2)}, u32[]{:S(2)}) collective-permute-start(f32[512,1024]{1,0:T(8,128)} %convolution_add_fusion), channel_id=1, source_target_pairs={{0,2},{1,3},{6,4},{7,5}} | collective-permute-start | bytes 6291464 | tf_op jit(solution)/shard_map/ppermute | solution.py:36
  271.2 74.0 %collective-permute-start.23 = (f32[512,1024]{1,0:T(8,128)}, f32[512,1024]{1,0:T(8,128)}, u32[]{:S(2)}, u32[]{:S(2)}) collective-permute-start(f32[512,1024]{1,0:T(8,128)} %convolution_add_fusion), channel_id=1, source_target_pairs={{2,4},{3,5},{4,2},{5,3}} | collective-permute-start | bytes 6291464 | tf_op jit(solution)/shard_map/ppermute | solution.py:36
  277.5 67.6 %collective-permute-start.21 = (f32[512,1024]{1,0:T(8,128)}, f32[512,1024]{1,0:T(8,128)}, u32[]{:S(2)}, u32[]{:S(2)}) collective-permute-start(f32[512,1024]{1,0:T(8,128)} %convolution_add_fusion.1), channel_id=1, source_target_pairs={{2,6},{3,7},{4,0},{5,1}} | collective-permute-start | bytes 6291464 | tf_op jit(solution)/shard_map/ppermute | solution.py:36
  286.8 51.6 %collective-permute-start.27 = (f32[256,512]{0,1:T(8,128)}, f32[256,512]{0,1:T(8,128)}, u32[]{:S(2)}, u32[]{:S(2)}) collective-permute-start(f32[256,512]{0,1:T(8,128)} %fusion.64), channel_id=1, source_target_pairs={{0,4},{1,5},{2,6},{3,7},{4,0},{5,1},{6,2},{7,3}} | collective-permute-start | bytes 1572872 | tf_op jit(solution)/shard_map/ppermute | solution.py:36
  344.4 38.5 %collective-permute-start.26 = (f32[256,1024]{1,0:T(8,128)S(1)}, f32[256,1024]{1,0:T(8,128)S(1)}, u32[]{:S(2)}, u32[]{:S(2)}) collective-permute-start(f32[256,1024]{1,0:T(8,128)S(1)} %get-tuple-element.22), channel_id=1, source_target_pairs={{0,1},{1,0},{2,3},{3,2},{4,5},{5,4},{6,7},{7,6}} | collective-permute-start | bytes 3145736 | tf_op jit(solution)/shard_map/ppermute | solution.py:36
  345.0 39.6 %collective-permute-start.25 = (f32[256,1024]{1,0:T(8,128)S(1)}, f32[256,1024]{1,0:T(8,128)S(1)}, u32[]{:S(2)}, u32[]{:S(2)}) collective-permute-start(f32[256,1024]{1,0:T(8,128)S(1)} %get-tuple-element.24), channel_id=1, source_target_pairs={{0,1},{1,0},{2,3},{3,2},{4,5},{5,4},{6,7},{7,6}} | collective-permute-start | bytes 3145736 | tf_op jit(solution)/shard_map/ppermute | solution.py:36
  345.2 5.3 %copy-start.12 = (f32[256,1024]{1,0:T(8,128)S(1)}, f32[256,1024]{1,0:T(8,128)}, u32[]{:S(2)}) copy-start(f32[256,1024]{1,0:T(8,128)} %get-tuple-element.16) | copy-start | bytes 3145732
  350.0 36.1 %collective-permute-start.24 = (f32[256,1024]{1,0:T(8,128)S(1)}, f32[256,1024]{1,0:T(8,128)S(1)}, u32[]{:S(2)}, u32[]{:S(2)}) collective-permute-start(f32[256,1024]{1,0:T(8,128)S(1)} %get-tuple-element.26), channel_id=1, source_target_pairs={{0,1},{1,0},{2,3},{3,2},{4,5},{5,4},{6,7},{7,6}} | collective-permute-start | bytes 3145736 | tf_op jit(solution)/shard_map/ppermute | solution.py:36
  (11 other events, 31.3 us)

commit v2 on v0

v2 whole, which is shorter than its diff:
```python
import functools

import jax
import jax.numpy as jnp
from jax import lax
from jax.experimental import pallas as pl
from jax.experimental.pallas import tpu as pltpu
from jax.sharding import PartitionSpec as P

BETA1 = 0.9
BETA2 = 0.9
EPS = 1e-8
LR = 0.1
STEP = 10
BIAS_ONE = 1.0 - BETA1 ** STEP
BIAS_TWO = 1.0 - BETA2 ** STEP

MESH = pl.DeviceIdType.MESH
F32, BF16 = jnp.float32, jnp.bfloat16
CHUNKS = 4
COPIES = 64


def _step(
    w_ref, g_ref, m_ref, v_ref, l_ref, r_ref, ql_ref, qr_ref,
    wo_ref, mo_ref, vo_ref, lo_ref, ro_ref,
    gat, acc, gbf, qrx, qro, part, precv, hbuf, qlb, qlt, mt, vt, wt, nbuf, kbuf, urecv, lbuf, qstage,
    ssem, rsem, lsem,
):
    y, r = lax.axis_index("col"), lax.axis_index("row")
    x, c = r // 2, r % 2
    diag = x == y
    off = x != y
    sel = jnp.where(diag, 0, 1)
    own, far = 2 * x, 2 * (1 - x)
    rx = 2 * (1 - x) + c
    rp = 2 * x + 1 - c
    rxp = 2 * (1 - x) + 1 - c
    mine = pl.ds(pl.multiple_of(c * 1024, 1024), 1024)
    other = pl.ds(pl.multiple_of((1 - c) * 1024, 1024), 1024)
    to_x, to_core, to_y, to_cross = (0, y, rx), (0, y, rp), (0, 1 - y, r), (0, 1 - y, rx)

    used = [0]
    local_used = [0]

    def remote(src, dst, dev):
        n = used[0]
        used[0] += 1
        return pltpu.make_async_remote_copy(
            src_ref=src, dst_ref=dst, send_sem=ssem.at[n], recv_sem=rsem.at[n], device_id=dev, device_id_type=MESH
        )

    def local(src, dst):
        n = local_used[0]
        local_used[0] += 1
        return pltpu.make_async_copy(src, dst, lsem.at[n])

    ld_g = local(g_ref, gat.at[0, r])
    ld_qr = local(qr_ref, acc)
    ld_ql = local(ql_ref, qstage)
    ld_m = local(m_ref.at[:, mine], mt.at[c])
    ld_v = local(v_ref.at[:, mine], vt.at[c])
    ld_w = local(w_ref.at[:, mine], wt.at[c])
    ld_l = local(l_ref, lbuf.at[0])
    for cp in (ld_ql, ld_qr, ld_g, ld_m, ld_v, ld_w, ld_l):
        cp.start()

    barrier = pltpu.get_barrier_semaphore()
    for dev in (to_x, to_core, to_y, to_cross):
        pl.semaphore_signal(barrier, inc=1, device_id=dev, device_id_type=MESH)
    pl.semaphore_wait(barrier, 4)

    def rows(k):
        return pl.ds(64 * k, 64)

    gx = [remote(g_ref.at[rows(k), :], gat.at[0, r, rows(k), :], to_x) for k in range(CHUNKS)]
    gp = remote(g_ref, gat.at[0, r], to_core)
    sm = remote(m_ref.at[:, other], mt.at[c], to_core)
    sv = remote(v_ref.at[:, other], vt.at[c], to_core)
    sw = remote(w_ref.at[:, other], wt.at[c], to_core)
    qcol = pl.ds(pl.multiple_of(y * 512, 512), 512)
    qx = remote(qlb.at[r, :, qcol], qlb.at[r, :, qcol], to_x)
    qya = remote(qlb.at[r, :, qcol], qlb.at[r, :, qcol], to_y)
    qyb = remote(qlb.at[rx, :, qcol], qlb.at[rx, :, qcol], to_y)
    qpa = remote(qlb.at[r], qlb.at[r], to_core)
    qpb = remote(qlb.at[rx], qlb.at[rx], to_core)
    qrp = remote(qro, qrx.at[c], to_core)
    gb = remote(gbf.at[:, :, mine], gbf.at[:, :, mine], to_y)
    fb = remote(gbf.at[:, :, mine], gbf.at[:, :, mine], to_core)
    gf = [remote(gat.at[0, rx, rows(k), :], gat.at[0, rx, rows(k), :], to_core) for k in range(CHUNKS)]
    y2 = [remote(gat.at[0, rx, rows(k), mine], gat.at[1, rx, rows(k), mine], to_y) for k in range(CHUNKS)]
    y3 = [remote(gat.at[0, rxp, rows(k), mine], gat.at[1, rxp, rows(k), mine], to_y) for k in range(CHUNKS)]
    f2 = [remote(gat.at[1, rx, rows(k), mine], gat.at[1, rx, rows(k), mine], to_core) for k in range(CHUNKS)]
    f3 = [remote(gat.at[1, rxp, rows(k), mine], gat.at[1, rxp, rows(k), mine], to_core) for k in range(CHUNKS)]
    ya = remote(gat.at[0, pl.ds(own, 2), :, mine], gat.at[1, pl.ds(own, 2), :, mine], to_y)

    def pslot(base, k):
        return part.at[base + k // 2, pl.ds(128 * (k % 2), 128), :]

    px = [remote(pslot(0, k), precv.at[k], to_x) for k in range(CHUNKS)]
    hx = [remote(hbuf.at[pl.ds(own, 2), rows(k), :], hbuf.at[pl.ds(own, 2), rows(k), :], to_x) for k in range(CHUNKS)]
    half = pl.ds(pl.multiple_of(x * 512, 512), 512)
    nx = [remote(nbuf.at[j, half, :], nbuf.at[j, half, :], to_x) for j in range(CHUNKS)]
    kp = [remote(kbuf.at[c, :, pl.ds(256 * j, 256)], kbuf.at[c, :, pl.ds(256 * j, 256)], to_core) for j in range(CHUNKS)]
    mo = remote(mt.at[1 - c], mo_ref.at[:, mine], to_core)
    vo = remote(vt.at[1 - c], vo_ref.at[:, mine], to_core)
    wo = remote(wt.at[1 - c], wo_ref.at[:, mine], to_core)
    order = [1 - c, c]
    ux = [remote(part.at[far + i], urecv.at[0, i], to_x) for i in order]
    uy = [remote(part.at[own + i], urecv.at[0, i], to_y) for i in order]
    uc = [remote(part.at[far + i], urecv.at[1, i], to_cross) for i in order]
    lx = remote(lbuf.at[1], lbuf.at[2], to_y)

    for cp in gx:
        cp.start()
    gp.start()
    ld_ql.wait()
    qlb[r, :, qcol] = qstage[...].astype(BF16)
    qya.start()
    qx.start()

    ld_qr.wait()

    def to_bf(t, carry):
        span = pl.ds(pl.multiple_of(t * 128, 128), 128)
        qro[span, :] = acc[span, other].astype(BF16)
        qrx[c, span, :] = acc[span, mine].astype(BF16)
        return carry

    lax.fori_loop(0, 8, to_bf, 0)
    qrp.start()
    ld_r = local(r_ref, acc)
    ld_r.start()

    ld_g.wait()
    gp.wait_recv()

    @pl.when(diag)
    def _():
        def cast(t, carry):
            span = pl.ds(pl.multiple_of(t * 64, 64), 64)
            for i in range(2):
                gbf[i, span, :] = gat[0, own + i, span, :].astype(BF16)
            return carry

        lax.fori_loop(0, 4, cast, 0)
        gb.start()

    sm.start()
    sv.start()
    sw.start()

    qrp.wait_recv()

    def inner(load, store):
        top, low = load(0), load(1)
        lhs = jnp.concatenate([top, low], 0)

        def cols(t, carry):
            span = pl.ds(pl.multiple_of(t * 256, 256), 256)
            value = jnp.dot(lhs[:, :1024], qrx[0, :, span], preferred_element_type=F32)
            value += jnp.dot(lhs[:, 1024:], qrx[1, :, span], preferred_element_type=F32)
            store(span, value)
            return carry

        lax.fori_loop(0, 4, cols, 0)

    def send_part(k):
        def store(span, value):
            part[k // 2, pl.ds(128 * (k % 2), 128), span] = value

        inner(lambda i: gat[sel, far + i, rows(k), :].astype(BF16), store)
        px[k].start()

    def relay(k):
        @pl.when(off)
        def _():
            y2[k].wait_recv()
            f2[k].start()
            y3[k].wait_recv()
            f3[k].start()
            f2[k].wait_recv()
            f3[k].wait_recv()

    for k in range(CHUNKS):
        gx[k].wait_recv()
        gf[k].start()

        @pl.when(diag)
        def _():
            y2[k].start()

        gf[k].wait_recv()

        @pl.when(diag)
        def _():
            y3[k].start()

        if k == 1:

            @pl.when(off)
            def _():
                gb.wait_recv()
                fb.start()

    qx.wait_recv()
    qyb.start()

    @pl.when(diag)
    def _():
        ya.start()

    @pl.when(off)
    def _():
        fb.wait_recv()

    def stat_right(base, t, last):
        lane = pl.ds(pl.multiple_of(c * 1024 + t * 256, 256), 256)
        tall = jnp.concatenate([gat[sel, base, :, lane], gat[sel, base + 1, :, lane]], 0).T
        span = pl.ds(pl.multiple_of(t * 256, 256), 256)

        def cols(n, carry):
            at = pl.ds(pl.multiple_of(n * 256, 256), 256)
            wide = jnp.concatenate([gat[0, base, :, at], gat[0, base + 1, :, at]], 0)
            value = jnp.dot(tall, wide, precision=lax.Precision.HIGHEST, preferred_element_type=F32)
            prev = acc[span, at]
            if not last:
                prev = BETA2 * prev
            acc[span, at] = prev + (1.0 - BETA2) * value
            return carry

        lax.fori_loop(0, 8, cols, 0)

    def stat_left(k):
        slot = jnp.where(y == k, 0, 1)
        for i in range(2):
            value = lax.dot_general(
                gat[0, r], gat[0, 2 * k + i], (((1,), (1,)), ((), ())), precision=lax.Precision.HIGHEST, preferred_element_type=F32
            )
            at = pl.ds(256 * i, 256)

            @pl.when(slot == 0)
            def _():
                lbuf[0, :, at] = BETA2 * lbuf[0, :, at] + (1.0 - BETA2) * value

            @pl.when(slot == 1)
            def _():
                lbuf[1, :, at] = value

    ld_r.wait()
    ld_l.wait()
    for k in range(CHUNKS):
        relay(k)
        send_part(k)

    def own_part(k):
        def store(span, value):
            part[2 + k // 2, pl.ds(128 * (k % 2), 128), span] = value

        inner(lambda i: gbf[i, rows(k), :], store)

    for k in range(CHUNKS):
        own_part(k)
    for k in range(CHUNKS):
        if k < 3:
            stat_right(far, k, False)
        px[k].wait_recv()
        for i in range(2):
            at = pl.ds(128 * (k % 2) + 64 * i, 64)
            hbuf[own + i, rows(k), :] = (part[2 + k // 2, at, :] + precv[k, pl.ds(64 * i, 64), :]).astype(BF16)
        hx[k].start()

    qya.wait_recv()
    qyb.wait_recv()
    qpa.start()
    qpb.start()
    qpa.wait_recv()
    qpb.wait_recv()

    def turn(t, carry):
        lane = pl.ds(pl.multiple_of(x * 512 + t * 128, 128), 128)
        for p in range(4):
            qlt[pl.ds(pl.multiple_of(t * 128, 128), 128), pl.ds(256 * p, 256)] = qlb[p, :, lane].astype(F32).T.astype(BF16)
        return carry

    lax.fori_loop(0, 4, turn, 0)
    stat_right(far, 3, False)
    ld_m.wait()
    ld_v.wait()
    ld_w.wait()
    sm.wait_recv()
    sv.wait_recv()
    sw.wait_recv()
    for k in range(CHUNKS):
        hx[k].wait_recv()

    for j in range(CHUNKS):
        at = pl.ds(256 * j, 256)
        for i in range(2):
            rot = jnp.zeros((256, 256), F32)
            for p in range(4):
                rot += jnp.dot(qlt[pl.ds(256 * i, 256), pl.ds(256 * p, 256)], hbuf[p, :, at], preferred_element_type=F32)
            first = BETA1 * mt[i, :, at] + (1.0 - BETA1) * rot
            second = BETA2 * vt[i, :, at] + (1.0 - BETA2) * rot * rot
            mt[i, :, at] = first
            vt[i, :, at] = second
            step = (first / BIAS_ONE) / (jnp.sqrt(second / BIAS_TWO) + EPS)
            nbuf[j, pl.ds(pl.multiple_of(x * 512 + 256 * i, 256), 256), :] = step.astype(BF16)
        nx[j].start()

    st_m = local(mt.at[c], mo_ref.at[:, mine])
    st_v = local(vt.at[c], vo_ref.at[:, mine])
    st_m.start()
    st_v.start()
    mo.start()
    vo.start()

    stat_left(0)
    stat_left(1)
    lx.start()

    def back(j):
        at = pl.ds(256 * j, 256)
        nx[j].wait_recv()

        def strip(p, carry):
            span = pl.ds(pl.multiple_of(p * 256, 256), 256)
            kbuf[c, span, at] = jnp.dot(qlb[p], nbuf[j], preferred_element_type=F32).astype(BF16)
            return carry

        lax.fori_loop(0, 4, strip, 0)
        kp[j].start()

    def update(p, lo, first):
        span = pl.ds(pl.multiple_of(p * 256, 256), 256)
        at = pl.ds(lo, 512)

        def cols(t, carry):
            lane = pl.ds(pl.multiple_of(t * 256, 256), 256)
            nt = (((1,), (1,)), ((), ()))
            value = lax.dot_general(kbuf[c, span, at], qrx[c, lane, at], nt, preferred_element_type=F32)
            value += lax.dot_general(kbuf[1 - c, span, at], qro[lane, at], nt, preferred_element_type=F32)
            part[p, :, lane] = value if first else part[p, :, lane] + value
            return carry

        lax.fori_loop(0, 4, cols, 0)

    for k in range(CHUNKS):
        px[k].wait_send()
    back(0)
    back(1)
    kp[0].wait_recv()
    kp[1].wait_recv()
    for i in range(4):
        update(i, 0, True)
    back(2)
    back(3)
    kp[2].wait_recv()
    kp[3].wait_recv()
    for n in range(2):
        update(far + order[n], 512, False)

        @pl.when(diag)
        def _():
            ux[n].start()

        @pl.when(off)
        def _():
            uc[n].start()

        update(own + order[n], 512, False)

        @pl.when(off)
        def _():
            uy[n].start()

    @pl.when(off)
    def _():
        ya.wait_recv()

    st_r = []
    for t in range(4):
        stat_right(own, t, True)
        cp = local(acc.at[pl.ds(256 * t, 256), :], ro_ref.at[pl.ds(256 * t, 256), :])
        cp.start()
        st_r.append(cp)
    lx.wait_recv()
    lbuf[0] = lbuf[0] + (1.0 - BETA2) * lbuf[2]
    st_l = local(lbuf.at[0], lo_ref)
    st_l.start()

    for n in range(2):
        i = order[n]

        @pl.when(diag)
        def _():
            uy[n].wait_recv()
            wt[i] = wt[i] - LR * (part[own + i] + urecv[0, i])

        @pl.when(off)
        def _():
            ux[n].wait_recv()
            uc[n].wait_recv()
            wt[i] = wt[i] - LR * (urecv[0, i] + urecv[1, i])

        if n == 0:
            wo.start()
        else:
            st_w = local(wt.at[c], wo_ref.at[:, mine])
            st_w.start()

    for cp in [*gx, gp, sm, sv, sw, qx, qya, qyb, qpa, qpb, qrp, *gf, *hx, *nx, *kp, lx]:
        cp.wait_send()

    @pl.when(diag)
    def _():
        for cp in [gb, *y2, *y3, ya, *ux]:
            cp.wait_send()

    @pl.when(off)
    def _():
        for cp in [fb, *f2, *f3, *uy, *uc]:
            cp.wait_send()

    for cp in (mo, vo, wo):
        cp.wait()
    for cp in (st_m, st_v, st_l, st_w, *st_r):
        cp.wait()


def solution(mesh):
    tile_spec = P(("layer", "row"), "col")

    def local_step(weight, grad_in, mom_first, mom_second, stat_left, stat_right, basis_left, basis_right):
        like = lambda a: jax.ShapeDtypeStruct(a.shape, a.dtype)
        return pl.pallas_call(
            _step,
            out_shape=(like(weight), like(mom_first), like(mom_second), like(stat_left), like(stat_right)),
            in_specs=[pl.BlockSpec(memory_space=pl.ANY)] * 8,
            out_specs=(pl.BlockSpec(memory_space=pl.ANY),) * 5,
            scratch_shapes=[
                pltpu.VMEM((2, 4, 256, 2048), F32),
                pltpu.VMEM((1024, 2048), F32),
                pltpu.VMEM((2, 256, 2048), BF16),
                pltpu.VMEM((2, 1024, 1024), BF16),
                pltpu.VMEM((1024, 1024), BF16),
                pltpu.VMEM((4, 256, 1024), F32),
                pltpu.VMEM((4, 128, 1024), F32),
                pltpu.VMEM((4, 256, 1024), BF16),
                pltpu.VMEM((4, 256, 1024), BF16),
                pltpu.VMEM((512, 1024), BF16),
                pltpu.VMEM((2, 256, 1024), F32),
                pltpu.VMEM((2, 256, 1024), F32),
                pltpu.VMEM((2, 256, 1024), F32),
                pltpu.VMEM((4, 1024, 256), BF16),
                pltpu.VMEM((2, 1024, 1024), BF16),
                pltpu.VMEM((2, 2, 256, 1024), F32),
                pltpu.VMEM((3, 256, 512), F32),
                pltpu.VMEM((256, 512), F32),
                pltpu.SemaphoreType.DMA((COPIES,)),
                pltpu.SemaphoreType.DMA((COPIES,)),
                pltpu.SemaphoreType.DMA((24,)),
            ],
            compiler_params=pltpu.CompilerParams(collective_id=0, has_side_effects=True, vmem_limit_bytes=67043328),
        )(weight, grad_in, mom_first, mom_second, stat_left, stat_right, basis_left, basis_right)

    return jax.shard_map(local_step, mesh=mesh, in_specs=(tile_spec,) * 8, out_specs=(tile_spec,) * 5, check_vma=False)
```

time: 673 us -> 221 us (0.33)
  waiting for transfers between devices: 520 us -> 0 us
  Pallas kernels: 0 us -> 208 us
  matrix products: 74.7 us -> 0 us
  other arithmetic: 29.7 us -> 0 us
  blocking collectives: 15.7 us -> 0 us
  between operations: 14.2 us -> 0.67 us
    reduce_scatter x4 -> x0, waiting for transfers between devices: 298 us -> none  [the longest x1 223 us: local_step(): lax.psum_scatter(right_part, 'row', scatter_dimension=0, tiled=True)]
    all_gather x4 -> x0, waiting for transfers between devices: 221 us -> none  [the longest x1 108 us: local_step(): lax.all_gather(basis_right.astype(jnp.bfloat16), 'row', axis=0, tiled=True)]
    pallas_call x0 -> x1, Pallas kernels: none -> 208 us  [local_step(): pl.pallas_call(_step, out_shape=(like(weight), like(mom_first), like(mom_...]
    dot_general x4 -> x0, matrix products: 74.7 us -> none  [the longest x1 31.6 us: local_step(): lax.dot_general(grad_rows, grad_in, contract_rows, precision=highest, pre...]
    all_gather x1 -> x0, blocking collectives: 15.7 us -> none  [local_step(): lax.all_gather(basis_left.astype(jnp.bfloat16), 'col', axis=1, tiled=True)]
    add x2 -> x0, other arithmetic: 14.1 us -> none  [the longest x1 12.1 us: local_step(): new_right = BETA2 * stat_right + (1.0 - BETA2) * right_sum]
    convert_element_type x3 -> x0, other arithmetic: 12.5 us -> none  [the longest x1 6.41 us: local_step(): direction.astype(jnp.bfloat16)]
    unnamed x14 -> x13, local copies, waits for them, and re-layouts: 17.2 us -> 11.8 us
  transfers between devices with their start and end apart: 8 -> 0, of which waited for: 7 -> 0; matrix products, arithmetic and copies ran while one was open for 14% -> 0% of each run, Pallas kernels for 0% -> 0%
where the time goes in v2:
time: 221 us; the launch traced here: 220 us
  Pallas kernels  208 us (94%)
  local copies, waits for them, and re-layouts  11.8 us (5%)
    pallas_call x1, Pallas kernels, local_step(): pl.pallas_call(_step, out_shape=(like(weight), like(mom_first), like(mom_...  208 us
    unnamed x13, local copies, waits for them, and re-layouts  11.8 us

profile of v2, /device:TPU:0, one launch (start us, length us, event | category | flops | bytes accessed | tf_op | source)
XLA Modules:
  0.0 220.4 jit_solution(6118035686493952927)
XLA Ops:
  0.6 208.0 %shard_map.119 = (f32[256,2048]{1,0:T(8,128)}, f32[256,2048]{1,0:T(8,128)}, f32[256,2048]{1,0:T(8,128)}, f32[256,512]{1,0:T(8,128)}, f32[1024,2048]{1,0:T(8,128)}) custom-call(f32[256,2048]{1,0:T(8,128)} %w_ref.1, f32[256,2048]{1,0:T(8,128)} %g_ref.1, f32[256,2048]{1,0:T(8,128)} %m_ref.1, f32[256,2048]{1,0:T(8,128)} %v_ref.1, f32[256,512]{1,0:T(8,128)} %l_ref.1, ...), custom_call_target="tpu_custom_call" | custom-call | tf_op jit(solution)/shard_map/pallas_call | solution.py:436
  208.6 0.0 copy-start.2
  208.7 0.0 copy-start.1
  208.7 0.0 copy-start.3
  208.7 3.3 %copy.18 = f32[256,2048]{1,0:T(8,128)} copy(f32[256,2048]{1,0:T(8,128)} %get-tuple-element.10) | data formatting | bytes 4194304
  212.0 0.0 copy-done.2
  212.0 0.0 copy-start
  212.0 1.3 copy.19
  213.3 0.0 copy-done.1
  213.3 1.3 copy.20
  214.6 0.0 copy-done.3
  214.6 0.8 copy.21
  215.4 1.6 copy-done
  217.1 3.4 %copy.22 = f32[1024,2048]{1,0:T(8,128)} copy(f32[1024,2048]{1,0:T(8,128)S(1)} %copy-done) | data formatting | bytes 16777216
Async XLA Ops:
  208.6 3.3 %copy-start.2 = (f32[256,2048]{1,0:T(8,128)S(1)}, f32[256,2048]{1,0:T(8,128)}, u32[]{:S(2)}) copy-start(f32[256,2048]{1,0:T(8,128)} %get-tuple-element.11) | copy-start | bytes 6291460
  208.7 4.6 %copy-start.1 = (f32[256,2048]{1,0:T(8,128)S(1)}, f32[256,2048]{1,0:T(8,128)}, u32[]{:S(2)}) copy-start(f32[256,2048]{1,0:T(8,128)} %get-tuple-element.12) | copy-start | bytes 6291460
  208.7 5.9 %copy-start.3 = (f32[256,512]{1,0:T(8,128)S(1)}, f32[256,512]{1,0:T(8,128)}, u32[]{:S(2)}) copy-start(f32[256,512]{1,0:T(8,128)} %get-tuple-element.13) | copy-start | bytes 1572868
  212.0 5.1 %copy-start = (f32[1024,2048]{1,0:T(8,128)S(1)}, f32[1024,2048]{1,0:T(8,128)}, u32[]{:S(2)}) copy-start(f32[1024,2048]{1,0:T(8,128)} %get-tuple-element.14) | copy-start | bytes 25165828

commit v3 on v2

v3 whole, which is shorter than its diff:
```python
import functools

import jax
import jax.numpy as jnp
from jax import lax
from jax.experimental import pallas as pl
from jax.experimental.pallas import tpu as pltpu
from jax.sharding import PartitionSpec as P

BETA1 = 0.9
BETA2 = 0.9
EPS = 1e-8
LR = 0.1
STEP = 10
BIAS_ONE = 1.0 - BETA1 ** STEP
BIAS_TWO = 1.0 - BETA2 ** STEP

MESH = pl.DeviceIdType.MESH
F32, BF16 = jnp.float32, jnp.bfloat16
CHUNKS = 4
COPIES = 80
GRANT = 51800000


def _step(
    w_ref, g_ref, m_ref, v_ref, l_ref, r_ref, ql_ref, qr_ref,
    wo, mo, vo, lo, acc,
    gat, qrx, qro, part, precv, hbuf, qlb, qlt, mt, vt, wt, nbuf, kbuf, urecv, lbuf,
    ssem, rsem, lsem,
):
    y, r = lax.axis_index("col"), lax.axis_index("row")
    x, c = r // 2, r % 2
    diag = x == y
    off = x != y
    sel = jnp.where(diag, 0, 1)
    own, far = 2 * x, 2 * (1 - x)
    rx = 2 * (1 - x) + c
    rp = 2 * x + 1 - c
    rxp = 2 * (1 - x) + 1 - c
    mine = pl.ds(pl.multiple_of(c * 1024, 1024), 1024)
    other = pl.ds(pl.multiple_of((1 - c) * 1024, 1024), 1024)
    to_x, to_core, to_y, to_cross = (0, y, rx), (0, y, rp), (0, 1 - y, r), (0, 1 - y, rx)

    nt = (((1,), (1,)), ((), ()))
    used = [0]
    local_used = [0]

    def remote(src, dst, dev):
        n = used[0]
        used[0] += 1
        return pltpu.make_async_remote_copy(
            src_ref=src, dst_ref=dst, send_sem=ssem.at[n], recv_sem=rsem.at[n], device_id=dev, device_id_type=MESH
        )

    def local(src, dst):
        n = local_used[0]
        local_used[0] += 1
        return pltpu.make_async_copy(src, dst, lsem.at[n])

    ld_g = local(g_ref, gat.at[0, r])
    ld_qr = local(qr_ref, acc)
    ld_ql = local(ql_ref, lo)
    ld_m = local(m_ref.at[:, mine], mo.at[:, mine])
    ld_v = local(v_ref.at[:, mine], vo.at[:, mine])
    ld_w = local(w_ref.at[:, mine], wo.at[:, mine])
    for cp in (ld_ql, ld_qr, ld_g, ld_m, ld_v, ld_w):
        cp.start()

    barrier = pltpu.get_barrier_semaphore()
    for dev in (to_x, to_core, to_y, to_cross):
        pl.semaphore_signal(barrier, inc=1, device_id=dev, device_id_type=MESH)
    pl.semaphore_wait(barrier, 4)

    def rows(k):
        return pl.ds(64 * k, 64)

    gx = [remote(g_ref.at[rows(k), :], gat.at[0, r, rows(k), :], to_x) for k in range(CHUNKS)]
    gp = remote(g_ref, gat.at[0, r], to_core)
    sm = remote(m_ref.at[:, other], mt, to_core)
    sv = remote(v_ref.at[:, other], vt, to_core)
    sw = remote(w_ref.at[:, other], wt, to_core)
    qcol = pl.ds(pl.multiple_of(y * 512, 512), 512)
    qx = remote(qlb.at[r, :, qcol], qlb.at[r, :, qcol], to_x)
    qya = remote(qlb.at[r, :, qcol], qlb.at[r, :, qcol], to_y)
    qyb = remote(qlb.at[rx, :, qcol], qlb.at[rx, :, qcol], to_y)
    qpa = remote(qlb.at[r], qlb.at[r], to_core)
    qpb = remote(qlb.at[rx], qlb.at[rx], to_core)
    qrp = remote(qro, qrx.at[c], to_core)
    gb = [remote(kbuf.at[c, pl.ds(0, 2), rows(k), :], kbuf.at[c, pl.ds(0, 2), rows(k), :], to_y) for k in range(CHUNKS)]
    fb = [remote(kbuf.at[c, pl.ds(0, 2), rows(k), :], kbuf.at[c, pl.ds(0, 2), rows(k), :], to_core) for k in range(CHUNKS)]
    gf = [remote(gat.at[0, rx, rows(k), :], gat.at[0, rx, rows(k), :], to_core) for k in range(CHUNKS)]
    y2 = [remote(gat.at[0, rx, rows(k), mine], gat.at[1, rx, rows(k), mine], to_y) for k in range(CHUNKS)]
    y3 = [remote(gat.at[0, rxp, rows(k), mine], gat.at[1, rxp, rows(k), mine], to_y) for k in range(CHUNKS)]
    f2 = [remote(gat.at[1, rx, rows(k), mine], gat.at[1, rx, rows(k), mine], to_core) for k in range(CHUNKS)]
    f3 = [remote(gat.at[1, rxp, rows(k), mine], gat.at[1, rxp, rows(k), mine], to_core) for k in range(CHUNKS)]
    ya = remote(gat.at[0, pl.ds(own, 2), :, mine], gat.at[1, pl.ds(own, 2), :, mine], to_y)

    def pslot(base, k):
        return part.at[base + k // 2, pl.ds(128 * (k % 2), 128), :]

    px = [remote(pslot(0, k), precv.at[k], to_x) for k in range(CHUNKS)]
    hx = [remote(hbuf.at[pl.ds(own, 2), rows(k), :], hbuf.at[pl.ds(own, 2), rows(k), :], to_x) for k in range(CHUNKS)]
    half = pl.ds(pl.multiple_of(x * 512, 512), 512)
    nx = [remote(nbuf.at[j, half, :], nbuf.at[j, half, :], to_x) for j in range(CHUNKS)]
    kp = [remote(kbuf.at[c, :, :, pl.ds(256 * j, 256)], kbuf.at[c, :, :, pl.ds(256 * j, 256)], to_core) for j in range(CHUNKS)]
    om = remote(mt, mo.at[:, mine], to_core)
    ov = remote(vt, vo.at[:, mine], to_core)
    order = [1 - c, c]

    def span(q):
        return pl.ds(128 * q, 128)

    ow = [remote(wt.at[span(q), :], wo.at[span(q), mine], to_core) for q in range(2)]
    pieces = [(n, q) for n in range(2) for q in range(2)]
    ux = [remote(part.at[far + order[n], span(q), :], urecv.at[0, order[n], span(q), :], to_x) for n, q in pieces]
    uy = [remote(part.at[own + order[n], span(q), :], urecv.at[0, order[n], span(q), :], to_y) for n, q in pieces]
    uc = [remote(part.at[far + order[n], span(q), :], urecv.at[1, order[n], span(q), :], to_cross) for n, q in pieces]
    lx = remote(lbuf.at[0], lbuf.at[1], to_y)

    for cp in gx:
        cp.start()
    gp.start()
    ld_ql.wait()
    qlb[r, :, qcol] = lo[...].astype(BF16)
    ld_l = local(l_ref, lo)
    ld_l.start()
    qya.start()
    qx.start()

    ld_qr.wait()

    def to_bf(t, carry):
        span = pl.ds(pl.multiple_of(t * 128, 128), 128)
        qro[span, :] = acc[span, other].astype(BF16)
        qrx[c, span, :] = acc[span, mine].astype(BF16)
        return carry

    lax.fori_loop(0, 8, to_bf, 0)
    qrp.start()
    ld_r = local(r_ref, acc)
    ld_r.start()

    ld_g.wait()
    gp.wait_recv()

    @pl.when(diag)
    def _():
        def cast(t, carry):
            span = pl.ds(pl.multiple_of(t * 64, 64), 64)
            for i in range(2):
                for h in range(2):
                    kbuf[h, i, span, :] = gat[0, own + i, span, pl.ds(1024 * h, 1024)].astype(BF16)
            return carry

        lax.fori_loop(0, 4, cast, 0)
        gb[0].start()

    sm.start()
    sv.start()
    sw.start()

    qrp.wait_recv()

    def inner(load, store):
        lhs = [jnp.concatenate([load(0, h), load(1, h)], 0) for h in range(2)]

        def cols(t, carry):
            span = pl.ds(pl.multiple_of(t * 256, 256), 256)
            value = jnp.dot(lhs[0], qrx[0, :, span], preferred_element_type=F32)
            value += jnp.dot(lhs[1], qrx[1, :, span], preferred_element_type=F32)
            store(span, value)
            return carry

        lax.fori_loop(0, 4, cols, 0)

    def send_part(k):
        def store(span, value):
            part[k // 2, pl.ds(128 * (k % 2), 128), span] = value

        inner(lambda i, h: gat[sel, far + i, rows(k), pl.ds(1024 * h, 1024)].astype(BF16), store)
        px[k].start()

    def relay(k):
        @pl.when(off)
        def _():
            y2[k].wait_recv()
            f2[k].start()
            y3[k].wait_recv()
            f3[k].start()
            f2[k].wait_recv()
            f3[k].wait_recv()

    for k in range(CHUNKS):
        gx[k].wait_recv()
        gf[k].start()

        @pl.when(diag)
        def _():
            y2[k].start()

        gf[k].wait_recv()

        @pl.when(diag)
        def _():
            y3[k].start()

        if k == CHUNKS - 1:

            @pl.when(diag)
            def _():
                for n in range(1, CHUNKS):
                    gb[n].start()

        if k > 0:
            relay(k - 1)
            send_part(k - 1)

    qx.wait_recv()
    qyb.start()

    @pl.when(diag)
    def _():
        ya.start()

    relay(CHUNKS - 1)
    send_part(CHUNKS - 1)

    def stat_right(base, t, last):
        lane = pl.ds(pl.multiple_of(c * 1024 + t * 256, 256), 256)
        tall = jnp.concatenate([gat[sel, base, :, lane], gat[sel, base + 1, :, lane]], 0).T
        span = pl.ds(pl.multiple_of(t * 256, 256), 256)

        def cols(n, carry):
            at = pl.ds(pl.multiple_of(n * 256, 256), 256)
            wide = jnp.concatenate([gat[0, base, :, at], gat[0, base + 1, :, at]], 0)
            value = jnp.dot(tall, wide, precision=lax.Precision.HIGHEST, preferred_element_type=F32)
            prev = acc[span, at]
            if not last:
                prev = BETA2 * prev
            acc[span, at] = prev + (1.0 - BETA2) * value
            return carry

        lax.fori_loop(0, 8, cols, 0)

    def gram(k):
        for i in range(2):
            def deep(t, value, i=i):
                lane = pl.ds(pl.multiple_of(t * 256, 256), 256)
                return value + lax.dot_general(
                    gat[0, r, :, lane], gat[0, 2 * k + i, :, lane], nt, precision=lax.Precision.HIGHEST, preferred_element_type=F32
                )

            yield pl.ds(256 * i, 256), lax.fori_loop(0, 8, deep, jnp.zeros((256, 256), F32))

    ld_r.wait()
    ld_l.wait()

    def own_part(k):
        def store(span, value):
            part[2 + k // 2, pl.ds(128 * (k % 2), 128), span] = value

        inner(lambda i, h: kbuf[h, i, rows(k), :], store)

    for k in range(CHUNKS):

        @pl.when(off)
        def _():
            gb[k].wait_recv()
            fb[k].start()
            fb[k].wait_recv()

        own_part(k)
        px[k].wait_recv()
        for i in range(2):
            at = pl.ds(128 * (k % 2) + 64 * i, 64)
            hbuf[own + i, rows(k), :] = (part[2 + k // 2, at, :] + precv[k, pl.ds(64 * i, 64), :]).astype(BF16)
        hx[k].start()
        if k < 3:
            stat_right(far, k, False)

    qya.wait_recv()
    qyb.wait_recv()

    @pl.when(diag)
    def _():
        for cp in gb:
            cp.wait_send()

    @pl.when(off)
    def _():
        for cp in fb:
            cp.wait_send()

    qpa.start()
    qpb.start()
    qpa.wait_recv()
    qpb.wait_recv()

    def turn(t, carry):
        lane = pl.ds(pl.multiple_of(x * 512 + t * 128, 128), 128)
        for p in range(4):
            qlt[pl.ds(pl.multiple_of(t * 128, 128), 128), pl.ds(256 * p, 256)] = qlb[p, :, lane].astype(F32).T.astype(BF16)
        return carry

    lax.fori_loop(0, 4, turn, 0)

    def basis_dot(t, base, at):
        value = jnp.zeros((128, at.size), F32)
        for i in range(2):
            lane = pl.ds(pl.multiple_of((base + i) * 256, 256), 256)
            value += jnp.dot(qlt[pl.ds(pl.multiple_of(t * 128, 128), 128), lane], hbuf[base + i, :, at], preferred_element_type=F32)
        return value

    def own_half(t, carry):
        for h in range(2):
            at = pl.ds(512 * h, 512)
            precv[t, :, at] = basis_dot(t, own, at)
        return carry

    lax.fori_loop(0, 4, own_half, 0)
    stat_right(far, 3, False)
    for at, value in gram(1 - y):
        lbuf[0, :, at] = value
    lx.start()
    ld_m.wait()
    ld_v.wait()
    ld_w.wait()
    sm.wait_recv()
    sv.wait_recv()
    sw.wait_recv()
    for k in range(CHUNKS):
        hx[k].wait_recv()

    for j in range(CHUNKS):
        at = pl.ds(256 * j, 256)
        lane = pl.ds(pl.multiple_of(c * 1024 + 256 * j, 256), 256)
        for n in range(2):
            i = order[n]
            mom, var, cols = (mt, vt, at) if n == 0 else (mo, vo, lane)
            for q in range(2):
                rot = precv[2 * i + q, :, at] + basis_dot(2 * i + q, far, at)
                first = BETA1 * mom[span(q), cols] + (1.0 - BETA1) * rot
                second = BETA2 * var[span(q), cols] + (1.0 - BETA2) * rot * rot
                mom[span(q), cols] = first
                var[span(q), cols] = second
                step = (first / BIAS_ONE) / (jnp.sqrt(second / BIAS_TWO) + EPS)
                nbuf[j, pl.ds(pl.multiple_of(x * 512 + 256 * i + 128 * q, 128), 128), :] = step.astype(BF16)
        nx[j].start()

    om.start()
    ov.start()

    def back(j):
        at = pl.ds(256 * j, 256)
        nx[j].wait_recv()

        for n in range(2):
            two = pl.ds(2 * n, 2)
            value = jnp.dot(qlb[two].reshape(512, 1024), nbuf[j], preferred_element_type=F32)
            kbuf[c, two, :, at] = value.astype(BF16).reshape(2, 256, 256)
        kp[j].start()

    def update(lo, width, first):
        at = pl.ds(lo, width)

        def cols(n, carry):
            lane, two = pl.ds(pl.multiple_of(n // 2 * 256, 256), 256), pl.ds(n % 2 * 2, 2)
            value = lax.dot_general(kbuf[c, two, :, at].reshape(512, width), qrx[c, lane, at], nt, preferred_element_type=F32)
            value += lax.dot_general(kbuf[1 - c, two, :, at].reshape(512, width), qro[lane, at], nt, preferred_element_type=F32)
            value = value.reshape(2, 256, 256)
            part[two, :, lane] = value if first else part[two, :, lane] + value
            return carry

        lax.fori_loop(0, 8, cols, 0)

    last = pl.ds(768, 256)

    def update_mine(n, carry):
        lane, two = pl.ds(pl.multiple_of(n // 2 * 256, 256), 256), pl.ds(n % 2 * 2, 2)
        value = lax.dot_general(kbuf[c, two, :, last].reshape(512, 256), qrx[c, lane, last], nt, preferred_element_type=F32)
        part[two, :, lane] += value.reshape(2, 256, 256)
        return carry

    def update_other(p, q):
        for t in range(4):
            lane = pl.ds(256 * t, 256)
            part[p, span(q), lane] += lax.dot_general(
                kbuf[1 - c, p, span(q), last], qro[lane, last], nt, preferred_element_type=F32
            )

    for k in range(CHUNKS):
        px[k].wait_send()
    back(0)
    back(1)
    kp[0].wait_recv()
    kp[1].wait_recv()
    update(0, 512, True)
    back(2)
    kp[2].wait_recv()
    update(512, 256, False)
    back(3)
    lax.fori_loop(0, 8, update_mine, 0)
    kp[3].wait_recv()
    for n, (m, q) in enumerate(pieces):
        update_other(far + order[m], q)

        @pl.when(diag)
        def _():
            ux[n].start()

        @pl.when(off)
        def _():
            uc[n].start()

        update_other(own + order[m], q)

        @pl.when(off)
        def _():
            uy[n].start()

    @pl.when(off)
    def _():
        ya.wait_recv()

    for t in range(4):
        stat_right(own, t, True)
    for at, value in gram(y):
        lo[:, at] = BETA2 * lo[:, at] + (1.0 - BETA2) * value
    lx.wait_recv()
    lo[...] = lo[...] + (1.0 - BETA2) * lbuf[1]

    for n, (m, q) in enumerate(pieces):
        i = order[m]
        out, cols = (wt, slice(None)) if m == 0 else (wo, mine)

        @pl.when(diag)
        def _():
            uy[n].wait_recv()
            out[span(q), cols] = out[span(q), cols] - LR * (part[own + i, span(q), :] + urecv[0, i, span(q), :])

        @pl.when(off)
        def _():
            ux[n].wait_recv()
            uc[n].wait_recv()
            out[span(q), cols] = out[span(q), cols] - LR * (urecv[0, i, span(q), :] + urecv[1, i, span(q), :])

        if m == 0:
            ow[q].start()

    for cp in [*gx, gp, sm, sv, sw, qx, qya, qyb, qpa, qpb, qrp, *gf, *hx, *nx, *kp, lx]:
        cp.wait_send()

    @pl.when(diag)
    def _():
        for cp in [*y2, *y3, ya, *ux]:
            cp.wait_send()

    @pl.when(off)
    def _():
        for cp in [*f2, *f3, *uy, *uc]:
            cp.wait_send()

    for cp in (om, ov, *ow):
        cp.wait()


def solution(mesh):
    tile_spec = P(("layer", "row"), "col")

    def local_step(weight, grad_in, mom_first, mom_second, stat_left, stat_right, basis_left, basis_right):
        like = lambda a: pltpu.VMEM(a.shape, a.dtype)
        return pl.pallas_call(
            _step,
            out_shape=(like(weight), like(mom_first), like(mom_second), like(stat_left), like(stat_right)),
            in_specs=[pl.BlockSpec(memory_space=pl.ANY)] * 8,
            out_specs=(pl.BlockSpec(memory_space=pltpu.VMEM),) * 5,
            scratch_shapes=[
                pltpu.VMEM((2, 4, 256, 2048), F32),
                pltpu.VMEM((2, 1024, 1024), BF16),
                pltpu.VMEM((1024, 1024), BF16),
                pltpu.VMEM((4, 256, 1024), F32),
                pltpu.VMEM((4, 128, 1024), F32),
                pltpu.VMEM((4, 256, 1024), BF16),
                pltpu.VMEM((4, 256, 1024), BF16),
                pltpu.VMEM((512, 1024), BF16),
                pltpu.VMEM((256, 1024), F32),
                pltpu.VMEM((256, 1024), F32),
                pltpu.VMEM((256, 1024), F32),
                pltpu.VMEM((4, 1024, 256), BF16),
                pltpu.VMEM((2, 4, 256, 1024), BF16),
                pltpu.VMEM((2, 2, 256, 1024), F32),
                pltpu.VMEM((2, 256, 512), F32),
                pltpu.SemaphoreType.DMA((COPIES,)),
                pltpu.SemaphoreType.DMA((COPIES,)),
                pltpu.SemaphoreType.DMA((24,)),
            ],
            compiler_params=pltpu.CompilerParams(collective_id=0, has_side_effects=True, vmem_limit_bytes=GRANT),
        )(weight, grad_in, mom_first, mom_second, stat_left, stat_right, basis_left, basis_right)

    return jax.shard_map(local_step, mesh=mesh, in_specs=(tile_spec,) * 8, out_specs=(tile_spec,) * 5, check_vma=False)
```

time: 221 us -> 210 us (0.950)
  Pallas kernels: 208 us -> 201 us
  local copies, waits for them, and re-layouts: 11.8 us -> 8.15 us
    pallas_call x1, Pallas kernels: 208 us -> 201 us  [local_step(): pl.pallas_call(_step, out_shape=(like(weight), like(mom_first), like(mom_...]
    unnamed x13 -> x5, local copies, waits for them, and re-layouts: 11.8 us -> 8.15 us
where the time goes in v3:
time: 210 us
  Pallas kernels  201 us (96%)
  local copies, waits for them, and re-layouts  8.15 us (4%)
    pallas_call x1, Pallas kernels, local_step(): pl.pallas_call(_step, out_shape=(like(weight), like(mom_first), like(mom_...  201 us
    unnamed x5, local copies, waits for them, and re-layouts  8.15 us

profile of v3, /device:TPU:0, one launch (start us, length us, event | category | flops | bytes accessed | tf_op | source)
XLA Modules:
  0.0 209.7 jit_solution(14329627127478768387)
XLA Ops:
  0.6 200.9 %shard_map.119 = (f32[256,2048]{1,0:T(8,128)S(1)}, f32[256,2048]{1,0:T(8,128)S(1)}, f32[256,2048]{1,0:T(8,128)S(1)}, f32[256,512]{1,0:T(8,128)S(1)}, f32[1024,2048]{1,0:T(8,128)S(1)}) custom-call(f32[256,2048]{1,0:T(8,128)} %w_ref.1, f32[256,2048]{1,0:T(8,128)} %g_ref.1, f32[256,2048]{1,0:T(8,128)} %m_ref.1, f32[256,2048]{1,0:T(8,128)} %v_ref.1, ...), custom_call_target="tpu_custom_call" | custom-call | tf_op jit(solution)/shard_map/pallas_call | solution.py:472
  201.5 1.3 copy.18
  202.9 0.8 copy.21
  203.7 1.3 copy.19
  205.0 1.3 copy.20
  206.3 3.4 %copy.22 = f32[1024,2048]{1,0:T(8,128)} copy(f32[1024,2048]{1,0:T(8,128)S(1)} %get-tuple-element.9) | data formatting | bytes 16777216

commit v4 on v3

--- a/solution.py
+++ b/solution.py
@@ -18,7 +18,7 @@
 MESH = pl.DeviceIdType.MESH
 F32, BF16 = jnp.float32, jnp.bfloat16
 CHUNKS = 4
-COPIES = 80
+COPIES = 84
 GRANT = 51800000
 
 
@@ -99,10 +99,13 @@
         return part.at[base + k // 2, pl.ds(128 * (k % 2), 128), :]
 
     px = [remote(pslot(0, k), precv.at[k], to_x) for k in range(CHUNKS)]
-    hx = [remote(hbuf.at[pl.ds(own, 2), rows(k), :], hbuf.at[pl.ds(own, 2), rows(k), :], to_x) for k in range(CHUNKS)]
+    hx = [remote(hbuf.at[pl.ds(own, 2), rows(k), :], hbuf.at[pl.ds(own, 2), rows(k), :], to_x) for k in range(CHUNKS - 1)]
+    tail = [(pl.ds(own, 2), rows(CHUNKS - 1), pl.ds(256 * j, 256)) for j in range(4)]
+    hc = [remote(hbuf.at[t], hbuf.at[t], to_x) for t in tail]
     half = pl.ds(pl.multiple_of(x * 512, 512), 512)
     nx = [remote(nbuf.at[j, half, :], nbuf.at[j, half, :], to_x) for j in range(CHUNKS)]
-    kp = [remote(kbuf.at[c, :, :, pl.ds(256 * j, 256)], kbuf.at[c, :, :, pl.ds(256 * j, 256)], to_core) for j in range(CHUNKS)]
+    kcut = [(c, pl.ds(base, 2), slice(None), pl.ds(256 * j, 256)) for j in range(CHUNKS) for base in (far, own)]
+    kp = [remote(kbuf.at[cut], kbuf.at[cut], to_core) for cut in kcut]
     om = remote(mt, mo.at[:, mine], to_core)
     ov = remote(vt, vo.at[:, mine], to_core)
     order = [1 - c, c]
@@ -274,9 +277,11 @@
         for i in range(2):
             at = pl.ds(128 * (k % 2) + 64 * i, 64)
             hbuf[own + i, rows(k), :] = (part[2 + k // 2, at, :] + precv[k, pl.ds(64 * i, 64), :]).astype(BF16)
-        hx[k].start()
-        if k < 3:
+        if k < CHUNKS - 1:
+            hx[k].start()
             stat_right(far, k, False)
+    for cp in hc:
+        cp.start()
 
     qya.wait_recv()
     qyb.wait_recv()
@@ -328,10 +333,11 @@
     sm.wait_recv()
     sv.wait_recv()
     sw.wait_recv()
-    for k in range(CHUNKS):
-        hx[k].wait_recv()
+    for cp in hx:
+        cp.wait_recv()
 
     for j in range(CHUNKS):
+        hc[j].wait_recv()
         at = pl.ds(256 * j, 256)
         lane = pl.ds(pl.multiple_of(c * 1024 + 256 * j, 256), 256)
         for n in range(2):
@@ -353,12 +359,11 @@
     def back(j):
         at = pl.ds(256 * j, 256)
         nx[j].wait_recv()
-
-        for n in range(2):
-            two = pl.ds(2 * n, 2)
+        for n, base in enumerate((far, own)):
+            two = pl.ds(base, 2)
             value = jnp.dot(qlb[two].reshape(512, 1024), nbuf[j], preferred_element_type=F32)
             kbuf[c, two, :, at] = value.astype(BF16).reshape(2, 256, 256)
-        kp[j].start()
+            kp[2 * j + n].start()
 
     def update(lo, width, first):
         at = pl.ds(lo, width)
@@ -392,15 +397,16 @@
         px[k].wait_send()
     back(0)
     back(1)
-    kp[0].wait_recv()
-    kp[1].wait_recv()
+    for cp in kp[:4]:
+        cp.wait_recv()
     update(0, 512, True)
     back(2)
-    kp[2].wait_recv()
+    for cp in kp[4:6]:
+        cp.wait_recv()
     update(512, 256, False)
     back(3)
     lax.fori_loop(0, 8, update_mine, 0)
-    kp[3].wait_recv()
+    kp[6].wait_recv()
     for n, (m, q) in enumerate(pieces):
         update_other(far + order[m], q)
 
@@ -412,6 +418,8 @@
         def _():
             uc[n].start()
 
+        if n == 0:
+            kp[7].wait_recv()
         update_other(own + order[m], q)
 
         @pl.when(off)
@@ -447,7 +455,7 @@
         if m == 0:
             ow[q].start()
 
-    for cp in [*gx, gp, sm, sv, sw, qx, qya, qyb, qpa, qpb, qrp, *gf, *hx, *nx, *kp, lx]:
+    for cp in [*gx, gp, sm, sv, sw, qx, qya, qyb, qpa, qpb, qrp, *gf, *hx, *hc, *nx, *kp, lx]:
         cp.wait_send()
 
     @pl.when(diag)
@@ -464,12 +472,22 @@
         cp.wait()
 
 
+def _write(*refs):
+    sems = refs[-1]
+    count = (len(refs) - 1) // 2
+    copies = [pltpu.make_async_copy(refs[n], refs[count + n], sems.at[n]) for n in range(count)]
+    for cp in copies:
+        cp.start()
+    for cp in copies:
+        cp.wait()
+
+
 def solution(mesh):
     tile_spec = P(("layer", "row"), "col")
 
     def local_step(weight, grad_in, mom_first, mom_second, stat_left, stat_right, basis_left, basis_right):
         like = lambda a: pltpu.VMEM(a.shape, a.dtype)
-        return pl.pallas_call(
+        outs = pl.pallas_call(
             _step,
             out_shape=(like(weight), like(mom_first), like(mom_second), like(stat_left), like(stat_right)),
             in_specs=[pl.BlockSpec(memory_space=pl.ANY)] * 8,
@@ -496,5 +514,13 @@
             ],
             compiler_params=pltpu.CompilerParams(collective_id=0, has_side_effects=True, vmem_limit_bytes=GRANT),
         )(weight, grad_in, mom_first, mom_second, stat_left, stat_right, basis_left, basis_right)
+        return pl.pallas_call(
+            _write,
+            out_shape=tuple(jax.ShapeDtypeStruct(o.shape, o.dtype) for o in outs),
+            in_specs=[pl.BlockSpec(memory_space=pltpu.VMEM)] * 5,
+            out_specs=(pl.BlockSpec(memory_space=pl.ANY),) * 5,
+            scratch_shapes=[pltpu.SemaphoreType.DMA((5,))],
+            compiler_params=pltpu.CompilerParams(vmem_limit_bytes=1048576),
+        )(*(pltpu.with_memory_space_constraint(o, pltpu.VMEM) for o in outs))
 
     return jax.shard_map(local_step, mesh=mesh, in_specs=(tile_spec,) * 8, out_specs=(tile_spec,) * 5, check_vma=False)

time: 210 us -> 206 us (0.981)
  local copies, waits for them, and re-layouts: 8.15 us -> 0 us
  Pallas kernels: 201 us -> 205 us
    unnamed x5 -> x0, local copies, waits for them, and re-layouts: 8.15 us -> none
    pallas_call x0 -> x1, Pallas kernels: none -> 5.61 us  [local_step(): pl.pallas_call(_write, out_shape=tuple((jax.ShapeDtypeStruct(o.shape, o.d...]
where the time goes in v4:
time: 206 us
  Pallas kernels  205 us (100%)
    pallas_call x1, Pallas kernels, local_step(): pl.pallas_call(_step, out_shape=(like(weight), like(mom_first), like(mom_...  199 us
    pallas_call x1, Pallas kernels, local_step(): pl.pallas_call(_write, out_shape=tuple((jax.ShapeDtypeStruct(o.shape, o.d...  5.61 us

profile of v4, /device:TPU:0, one launch (start us, length us, event | category | flops | bytes accessed | tf_op | source)
XLA Modules:
  0.0 205.9 jit_solution(14709986004079096640)
XLA Ops:
  0.6 199.5 %shard_map.119 = (f32[256,2048]{1,0:T(8,128)S(1)}, f32[256,2048]{1,0:T(8,128)S(1)}, f32[256,2048]{1,0:T(8,128)S(1)}, f32[256,512]{1,0:T(8,128)S(1)}, f32[1024,2048]{1,0:T(8,128)S(1)}) custom-call(f32[256,2048]{1,0:T(8,128)} %w_ref.1, f32[256,2048]{1,0:T(8,128)} %g_ref.1, f32[256,2048]{1,0:T(8,128)} %m_ref.1, f32[256,2048]{1,0:T(8,128)} %v_ref.1, ...), custom_call_target="tpu_custom_call" | custom-call | tf_op jit(solution)/shard_map/pallas_call | solution.py:490
  200.1 5.6 %shard_map.120 = (f32[256,2048]{1,0:T(8,128)}, f32[256,2048]{1,0:T(8,128)}, f32[256,2048]{1,0:T(8,128)}, f32[256,512]{1,0:T(8,128)}, f32[1024,2048]{1,0:T(8,128)}) custom-call(f32[256,2048]{1,0:T(8,128)S(1)} %get-tuple-element.10.refs_0_, f32[256,2048]{1,0:T(8,128)S(1)} %get-tuple-element.11.refs_1_, f32[256,2048]{1,0:T(8,128)S(1)} %get-tuple-element.12.refs_2_, ...), custom_call_target="tpu_custom_call" | custom-call | tf_op jit(solution)/shard_map/pallas_call | solution.py:517

commit v5 on v4

--- a/solution.py
+++ b/solution.py
@@ -18,7 +18,8 @@
 MESH = pl.DeviceIdType.MESH
 F32, BF16 = jnp.float32, jnp.bfloat16
 CHUNKS = 4
-COPIES = 84
+COPIES = 83
+UNROLL = 2
 GRANT = 51800000
 
 
@@ -365,26 +366,20 @@
             kbuf[c, two, :, at] = value.astype(BF16).reshape(2, 256, 256)
             kp[2 * j + n].start()
 
-    def update(lo, width, first):
+    def update(lo, width, near, first=False):
         at = pl.ds(lo, width)
+        core, basis = (c, qrx.at[c]) if near else (1 - c, qro)
 
         def cols(n, carry):
             lane, two = pl.ds(pl.multiple_of(n // 2 * 256, 256), 256), pl.ds(n % 2 * 2, 2)
-            value = lax.dot_general(kbuf[c, two, :, at].reshape(512, width), qrx[c, lane, at], nt, preferred_element_type=F32)
-            value += lax.dot_general(kbuf[1 - c, two, :, at].reshape(512, width), qro[lane, at], nt, preferred_element_type=F32)
+            value = lax.dot_general(kbuf[core, two, :, at].reshape(512, width), basis[lane, at], nt, preferred_element_type=F32)
             value = value.reshape(2, 256, 256)
             part[two, :, lane] = value if first else part[two, :, lane] + value
             return carry
 
-        lax.fori_loop(0, 8, cols, 0)
+        lax.fori_loop(0, 8, cols, 0, unroll=UNROLL)
 
     last = pl.ds(768, 256)
-
-    def update_mine(n, carry):
-        lane, two = pl.ds(pl.multiple_of(n // 2 * 256, 256), 256), pl.ds(n % 2 * 2, 2)
-        value = lax.dot_general(kbuf[c, two, :, last].reshape(512, 256), qrx[c, lane, last], nt, preferred_element_type=F32)
-        part[two, :, lane] += value.reshape(2, 256, 256)
-        return carry
 
     def update_other(p, q):
         for t in range(4):
@@ -396,16 +391,19 @@
     for k in range(CHUNKS):
         px[k].wait_send()
     back(0)
+    update(0, 256, True, True)
     back(1)
+    update(256, 256, True)
     for cp in kp[:4]:
         cp.wait_recv()
-    update(0, 512, True)
+    update(0, 512, False)
     back(2)
+    update(512, 256, True)
     for cp in kp[4:6]:
         cp.wait_recv()
     update(512, 256, False)
     back(3)
-    lax.fori_loop(0, 8, update_mine, 0)
+    update(768, 256, True)
     kp[6].wait_recv()
     for n, (m, q) in enumerate(pieces):
         update_other(far + order[m], q)
@@ -475,7 +473,13 @@
 def _write(*refs):
     sems = refs[-1]
     count = (len(refs) - 1) // 2
-    copies = [pltpu.make_async_copy(refs[n], refs[count + n], sems.at[n]) for n in range(count)]
+    copies = []
+    for n in range(count):
+        rows = refs[n].shape[0]
+        size = min(rows, 128)
+        for lo in range(0, rows, size):
+            cut = pl.ds(lo, size)
+            copies.append(pltpu.make_async_copy(refs[n].at[cut, :], refs[count + n].at[cut, :], sems.at[len(copies)]))
     for cp in copies:
         cp.start()
     for cp in copies:
@@ -510,7 +514,7 @@
                 pltpu.VMEM((2, 256, 512), F32),
                 pltpu.SemaphoreType.DMA((COPIES,)),
                 pltpu.SemaphoreType.DMA((COPIES,)),
-                pltpu.SemaphoreType.DMA((24,)),
+                pltpu.SemaphoreType.DMA((8,)),
             ],
             compiler_params=pltpu.CompilerParams(collective_id=0, has_side_effects=True, vmem_limit_bytes=GRANT),
         )(weight, grad_in, mom_first, mom_second, stat_left, stat_right, basis_left, basis_right)
@@ -519,7 +523,7 @@
             out_shape=tuple(jax.ShapeDtypeStruct(o.shape, o.dtype) for o in outs),
             in_specs=[pl.BlockSpec(memory_space=pltpu.VMEM)] * 5,
             out_specs=(pl.BlockSpec(memory_space=pl.ANY),) * 5,
-            scratch_shapes=[pltpu.SemaphoreType.DMA((5,))],
+            scratch_shapes=[pltpu.SemaphoreType.DMA((16,))],
             compiler_params=pltpu.CompilerParams(vmem_limit_bytes=1048576),
         )(*(pltpu.with_memory_space_constraint(o, pltpu.VMEM) for o in outs))
 

time: 206 us -> 204 us (level)
  no operation moved by 1% of the time
where the time goes in v5:
time: 204 us
  Pallas kernels  203 us (100%)
    pallas_call x1, Pallas kernels, local_step(): pl.pallas_call(_step, out_shape=(like(weight), like(mom_first), like(mom_...  198 us
    pallas_call x1, Pallas kernels, local_step(): pl.pallas_call(_write, out_shape=tuple((jax.ShapeDtypeStruct(o.shape, o.d...  5.49 us

profile of v5, /device:TPU:0, one launch (start us, length us, event | category | flops | bytes accessed | tf_op | source)
XLA Modules:
  0.0 203.8 jit_solution(14562597713515488014)
XLA Ops:
  0.6 197.5 %shard_map.119 = (f32[256,2048]{1,0:T(8,128)S(1)}, f32[256,2048]{1,0:T(8,128)S(1)}, f32[256,2048]{1,0:T(8,128)S(1)}, f32[256,512]{1,0:T(8,128)S(1)}, f32[1024,2048]{1,0:T(8,128)S(1)}) custom-call(f32[256,2048]{1,0:T(8,128)} %w_ref.1, f32[256,2048]{1,0:T(8,128)} %g_ref.1, f32[256,2048]{1,0:T(8,128)} %m_ref.1, f32[256,2048]{1,0:T(8,128)} %v_ref.1, ...), custom_call_target="tpu_custom_call" | custom-call | tf_op jit(solution)/shard_map/pallas_call | solution.py:494
  198.2 5.5 %shard_map.120 = (f32[256,2048]{1,0:T(8,128)}, f32[256,2048]{1,0:T(8,128)}, f32[256,2048]{1,0:T(8,128)}, f32[256,512]{1,0:T(8,128)}, f32[1024,2048]{1,0:T(8,128)}) custom-call(f32[256,2048]{1,0:T(8,128)S(1)} %get-tuple-element.10.refs_0_, f32[256,2048]{1,0:T(8,128)S(1)} %get-tuple-element.11.refs_1_, f32[256,2048]{1,0:T(8,128)S(1)} %get-tuple-element.12.refs_2_, ...), custom_call_target="tpu_custom_call" | custom-call | tf_op jit(solution)/shard_map/pallas_call | solution.py:521

commit v6 on v5

--- a/solution.py
+++ b/solution.py
@@ -46,17 +46,26 @@
     used = [0]
     local_used = [0]
 
-    def remote(src, dst, dev):
+    sends = [0]
+
+    def remote(src, dst, dev, lane=None):
         n = used[0]
         used[0] += 1
+        if lane is None:
+            lane = sends[0]
+            sends[0] += 1
         return pltpu.make_async_remote_copy(
-            src_ref=src, dst_ref=dst, send_sem=ssem.at[n], recv_sem=rsem.at[n], device_id=dev, device_id_type=MESH
+            src_ref=src, dst_ref=dst, send_sem=ssem.at[lane], recv_sem=rsem.at[n], device_id=dev, device_id_type=MESH
         )
 
     def local(src, dst):
         n = local_used[0]
         local_used[0] += 1
         return pltpu.make_async_copy(src, dst, lsem.at[n])
+
+    barrier = pltpu.get_barrier_semaphore()
+    for dev in (to_x, to_core, to_y, to_cross):
+        pl.semaphore_signal(barrier, inc=1, device_id=dev, device_id_type=MESH)
 
     ld_g = local(g_ref, gat.at[0, r])
     ld_qr = local(qr_ref, acc)
@@ -67,9 +76,6 @@
     for cp in (ld_ql, ld_qr, ld_g, ld_m, ld_v, ld_w):
         cp.start()
 
-    barrier = pltpu.get_barrier_semaphore()
-    for dev in (to_x, to_core, to_y, to_cross):
-        pl.semaphore_signal(barrier, inc=1, device_id=dev, device_id_type=MESH)
     pl.semaphore_wait(barrier, 4)
 
     def rows(k):
@@ -87,13 +93,15 @@
     qpa = remote(qlb.at[r], qlb.at[r], to_core)
     qpb = remote(qlb.at[rx], qlb.at[rx], to_core)
     qrp = remote(qro, qrx.at[c], to_core)
+    lane = sends[0]
     gb = [remote(kbuf.at[c, pl.ds(0, 2), rows(k), :], kbuf.at[c, pl.ds(0, 2), rows(k), :], to_y) for k in range(CHUNKS)]
-    fb = [remote(kbuf.at[c, pl.ds(0, 2), rows(k), :], kbuf.at[c, pl.ds(0, 2), rows(k), :], to_core) for k in range(CHUNKS)]
+    fb = [remote(kbuf.at[c, pl.ds(0, 2), rows(k), :], kbuf.at[c, pl.ds(0, 2), rows(k), :], to_core, lane + k) for k in range(CHUNKS)]
     gf = [remote(gat.at[0, rx, rows(k), :], gat.at[0, rx, rows(k), :], to_core) for k in range(CHUNKS)]
+    lane = sends[0]
     y2 = [remote(gat.at[0, rx, rows(k), mine], gat.at[1, rx, rows(k), mine], to_y) for k in range(CHUNKS)]
     y3 = [remote(gat.at[0, rxp, rows(k), mine], gat.at[1, rxp, rows(k), mine], to_y) for k in range(CHUNKS)]
-    f2 = [remote(gat.at[1, rx, rows(k), mine], gat.at[1, rx, rows(k), mine], to_core) for k in range(CHUNKS)]
-    f3 = [remote(gat.at[1, rxp, rows(k), mine], gat.at[1, rxp, rows(k), mine], to_core) for k in range(CHUNKS)]
+    f2 = [remote(gat.at[1, rx, rows(k), mine], gat.at[1, rx, rows(k), mine], to_core, lane + k) for k in range(CHUNKS)]
+    f3 = [remote(gat.at[1, rxp, rows(k), mine], gat.at[1, rxp, rows(k), mine], to_core, lane + 4 + k) for k in range(CHUNKS)]
     ya = remote(gat.at[0, pl.ds(own, 2), :, mine], gat.at[1, pl.ds(own, 2), :, mine], to_y)
 
     def pslot(base, k):
@@ -116,9 +124,10 @@
 
     ow = [remote(wt.at[span(q), :], wo.at[span(q), mine], to_core) for q in range(2)]
     pieces = [(n, q) for n in range(2) for q in range(2)]
+    lane = sends[0]
     ux = [remote(part.at[far + order[n], span(q), :], urecv.at[0, order[n], span(q), :], to_x) for n, q in pieces]
     uy = [remote(part.at[own + order[n], span(q), :], urecv.at[0, order[n], span(q), :], to_y) for n, q in pieces]
-    uc = [remote(part.at[far + order[n], span(q), :], urecv.at[1, order[n], span(q), :], to_cross) for n, q in pieces]
+    uc = [remote(part.at[far + order[n], span(q), :], urecv.at[1, order[n], span(q), :], to_cross, lane + 2 * n + q) for n, q in pieces]
     lx = remote(lbuf.at[0], lbuf.at[1], to_y)
 
     for cp in gx:
@@ -512,7 +521,7 @@
                 pltpu.VMEM((2, 4, 256, 1024), BF16),
                 pltpu.VMEM((2, 2, 256, 1024), F32),
                 pltpu.VMEM((2, 256, 512), F32),
-                pltpu.SemaphoreType.DMA((COPIES,)),
+                pltpu.SemaphoreType.DMA((COPIES - 16,)),
                 pltpu.SemaphoreType.DMA((COPIES,)),
                 pltpu.SemaphoreType.DMA((8,)),
             ],

time: 204 us -> 204 us (level)
  no operation moved by 1% of the time
where the time goes in v6:
time: 204 us
  Pallas kernels  203 us (100%)
    pallas_call x1, Pallas kernels, local_step(): pl.pallas_call(_step, out_shape=(like(weight), like(mom_first), like(mom_...  197 us
    pallas_call x1, Pallas kernels, local_step(): pl.pallas_call(_write, out_shape=tuple((jax.ShapeDtypeStruct(o.shape, o.d...  5.49 us

profile of v6, /device:TPU:0, one launch (start us, length us, event | category | flops | bytes accessed | tf_op | source)
XLA Modules:
  0.0 203.7 jit_solution(9833822044605621872)
XLA Ops:
  0.6 197.4 %shard_map.119 = (f32[256,2048]{1,0:T(8,128)S(1)}, f32[256,2048]{1,0:T(8,128)S(1)}, f32[256,2048]{1,0:T(8,128)S(1)}, f32[256,512]{1,0:T(8,128)S(1)}, f32[1024,2048]{1,0:T(8,128)S(1)}) custom-call(f32[256,2048]{1,0:T(8,128)} %w_ref.1, f32[256,2048]{1,0:T(8,128)} %g_ref.1, f32[256,2048]{1,0:T(8,128)} %m_ref.1, f32[256,2048]{1,0:T(8,128)} %v_ref.1, ...), custom_call_target="tpu_custom_call" | custom-call | tf_op jit(solution)/shard_map/pallas_call | solution.py:503
  198.0 5.5 %shard_map.120 = (f32[256,2048]{1,0:T(8,128)}, f32[256,2048]{1,0:T(8,128)}, f32[256,2048]{1,0:T(8,128)}, f32[256,512]{1,0:T(8,128)}, f32[1024,2048]{1,0:T(8,128)}) custom-call(f32[256,2048]{1,0:T(8,128)S(1)} %get-tuple-element.10.refs_0_, f32[256,2048]{1,0:T(8,128)S(1)} %get-tuple-element.11.refs_1_, f32[256,2048]{1,0:T(8,128)S(1)} %get-tuple-element.12.refs_2_, ...), custom_call_target="tpu_custom_call" | custom-call | tf_op jit(solution)/shard_map/pallas_call | solution.py:530

commit v7 on v6

--- a/solution.py
+++ b/solution.py
@@ -81,7 +81,12 @@
     def rows(k):
         return pl.ds(64 * k, 64)
 
-    gx = [remote(g_ref.at[rows(k), :], gat.at[0, r, rows(k), :], to_x) for k in range(CHUNKS)]
+    lane = sends[0]
+    sends[0] += 1
+    gx = [remote(g_ref.at[rows(k), :], gat.at[0, r, rows(k), :], to_x, lane) for k in range(CHUNKS)]
+    gx_all = pltpu.make_async_remote_copy(
+        src_ref=g_ref, dst_ref=gat.at[0, r], send_sem=ssem.at[lane], recv_sem=rsem.at[0], device_id=to_x, device_id_type=MESH
+    )
     gp = remote(g_ref, gat.at[0, r], to_core)
     sm = remote(m_ref.at[:, other], mt, to_core)
     sv = remote(v_ref.at[:, other], vt, to_core)
@@ -462,7 +467,7 @@
         if m == 0:
             ow[q].start()
 
-    for cp in [*gx, gp, sm, sv, sw, qx, qya, qyb, qpa, qpb, qrp, *gf, *hx, *hc, *nx, *kp, lx]:
+    for cp in [gx_all, gp, sm, sv, sw, qx, qya, qyb, qpa, qpb, qrp, *gf, *hx, *hc, *nx, *kp, lx]:
         cp.wait_send()
 
     @pl.when(diag)
@@ -521,7 +526,7 @@
                 pltpu.VMEM((2, 4, 256, 1024), BF16),
                 pltpu.VMEM((2, 2, 256, 1024), F32),
                 pltpu.VMEM((2, 256, 512), F32),
-                pltpu.SemaphoreType.DMA((COPIES - 16,)),
+                pltpu.SemaphoreType.DMA((COPIES - 19,)),
                 pltpu.SemaphoreType.DMA((COPIES,)),
                 pltpu.SemaphoreType.DMA((8,)),
             ],

time: 204 us -> 204 us (level)
  no operation moved by 1% of the time
where the time goes in v7:
time: 204 us
  Pallas kernels  203 us (100%)
    pallas_call x1, Pallas kernels, local_step(): pl.pallas_call(_step, out_shape=(like(weight), like(mom_first), like(mom_...  197 us
    pallas_call x1, Pallas kernels, local_step(): pl.pallas_call(_write, out_shape=tuple((jax.ShapeDtypeStruct(o.shape, o.d...  5.49 us

profile of v7, /device:TPU:0, one launch (start us, length us, event | category | flops | bytes accessed | tf_op | source)
XLA Modules:
  0.0 203.6 jit_solution(14730813983867362189)
XLA Ops:
  0.6 197.3 %shard_map.119 = (f32[256,2048]{1,0:T(8,128)S(1)}, f32[256,2048]{1,0:T(8,128)S(1)}, f32[256,2048]{1,0:T(8,128)S(1)}, f32[256,512]{1,0:T(8,128)S(1)}, f32[1024,2048]{1,0:T(8,128)S(1)}) custom-call(f32[256,2048]{1,0:T(8,128)} %w_ref.1, f32[256,2048]{1,0:T(8,128)} %g_ref.1, f32[256,2048]{1,0:T(8,128)} %m_ref.1, f32[256,2048]{1,0:T(8,128)} %v_ref.1, ...), custom_call_target="tpu_custom_call" | custom-call | tf_op jit(solution)/shard_map/pallas_call | solution.py:508
  198.0 5.5 %shard_map.120 = (f32[256,2048]{1,0:T(8,128)}, f32[256,2048]{1,0:T(8,128)}, f32[256,2048]{1,0:T(8,128)}, f32[256,512]{1,0:T(8,128)}, f32[1024,2048]{1,0:T(8,128)}) custom-call(f32[256,2048]{1,0:T(8,128)S(1)} %get-tuple-element.10.refs_0_, f32[256,2048]{1,0:T(8,128)S(1)} %get-tuple-element.11.refs_1_, f32[256,2048]{1,0:T(8,128)S(1)} %get-tuple-element.12.refs_2_, ...), custom_call_target="tpu_custom_call" | custom-call | tf_op jit(solution)/shard_map/pallas_call | solution.py:535
